TPU v7x, 16 devices: a whole 2x2x2 slice. The times are simulated.
16 devices in a mesh: fsdp: 16 (over z, y, x, core).
Axes of the slice: x: 2, y: 2, z: 2, core: 2. Of those that a mesh axis runs over, the one named last changes fastest.
Arguments:
- tokens: int32 [16, 1024], P('fsdp')
- labels: int32 [16, 1024], P('fsdp')
- loss_mask: int32 [16, 1024], P('fsdp')
- hidden: bfloat16 [16, 1024, 960], P('fsdp')
- d_emb: bfloat16 [16, 1024, 960], P('fsdp')
- embed_table: bfloat16 [49152, 960], P('fsdp')
- ln_gain: float32 [960], P('fsdp')
- ln_bias: float32 [960], P('fsdp')
Outputs:
- output 1: bfloat16 [16, 1024, 960], P('fsdp')
- output 2: float32 [], replicated
- output 3: bfloat16 [16, 1024, 960], P('fsdp')
- output 4: float32 [49152, 960], P('fsdp')
- output 5: float32 [960], P('fsdp')
- output 6: float32 [960], P('fsdp')
All inputs are finite; a program needn't handle non-finite values.
Results may differ from a plain program's by a relative error of at most 0.001.
Values are sent between devices in bfloat16 or wider.
A program may use at most 1 GiB of HBM per device.

v0:
```python
import jax
import jax.numpy as jnp
from jax import lax
from jax.sharding import PartitionSpec as P

LN_EPSILON = 1e-5


def layer_norm(inputs, ln_gain, ln_bias):
    row_mean = jnp.mean(inputs, axis=-1, keepdims=True)
    centred = inputs - row_mean
    row_var = jnp.mean(centred * centred, axis=-1, keepdims=True)
    return centred * lax.rsqrt(row_var + LN_EPSILON) * ln_gain + ln_bias


def solution(mesh):
    batch_spec = P('fsdp', None)
    act_spec = P('fsdp', None, None)
    vec_spec = P('fsdp')

    def device_step(tokens, labels, loss_mask, hidden, d_emb, table_shard, gain_shard, bias_shard):
        n_rows, seq_len, model_dim = hidden.shape
        embed_table = lax.all_gather(table_shard, 'fsdp', axis=0, tiled=True)
        ln_gain = lax.all_gather(gain_shard, 'fsdp', axis=0, tiled=True)
        ln_bias = lax.all_gather(bias_shard, 'fsdp', axis=0, tiled=True)
        mask_count = lax.psum(jnp.sum(loss_mask.astype(jnp.float32)), 'fsdp')
        vocab_size = embed_table.shape[0]
        tok_flat = tokens.reshape(-1)
        label_flat = labels.reshape(-1)
        weight = loss_mask.reshape(-1).astype(jnp.float32) / mask_count
        emb_rows = jnp.take(embed_table, tok_flat, axis=0).reshape(n_rows, seq_len, model_dim)
        normed, ln_vjp = jax.vjp(layer_norm, hidden.reshape(-1, model_dim).astype(jnp.float32), ln_gain, ln_bias)
        normed_bf = normed.astype(jnp.bfloat16)
        logits = lax.dot_general(normed_bf, embed_table, (((1,), (1,)), ((), ())), preferred_element_type=jnp.float32)
        log_norm = jax.nn.logsumexp(logits, axis=1)
        label_hit = label_flat[:, None] == jnp.arange(vocab_size, dtype=jnp.int32)[None, :]
        label_logit = jnp.sum(jnp.where(label_hit, logits, 0.0), axis=1)
        mean_loss = lax.psum(jnp.sum(weight * (log_norm - label_logit)), 'fsdp')
        soft_probs = jnp.exp(logits - log_norm[:, None])
        d_logits = (weight[:, None] * (soft_probs - label_hit.astype(jnp.float32))).astype(jnp.bfloat16)
        d_normed = jnp.dot(d_logits, embed_table, preferred_element_type=jnp.float32)
        d_hidden, d_gain, d_bias = ln_vjp(d_normed)
        d_table = lax.dot_general(d_logits, normed_bf, (((0,), (0,)), ((), ())), preferred_element_type=jnp.float32)
        d_table = d_table.at[tok_flat].add(d_emb.reshape(-1, model_dim).astype(jnp.float32))
        d_table_shard = lax.psum_scatter(d_table, 'fsdp', scatter_dimension=0, tiled=True)
        d_gain_shard = lax.psum_scatter(d_gain, 'fsdp', scatter_dimension=0, tiled=True)
        d_bias_shard = lax.psum_scatter(d_bias, 'fsdp', scatter_dimension=0, tiled=True)
        d_hidden = d_hidden.astype(jnp.bfloat16).reshape(n_rows, seq_len, model_dim)
        return (emb_rows, mean_loss, d_hidden, d_table_shard, d_gain_shard, d_bias_shard)

    return jax.shard_map(device_step, mesh=mesh, in_specs=(batch_spec, batch_spec, batch_spec, act_spec, act_spec, batch_spec, vec_spec, vec_spec), out_specs=(act_spec, P(), act_spec, batch_spec, vec_spec, vec_spec), check_vma=False)
```

profile of v0, /device:TPU:0, one launch (start us, length us, event | category | flops | bytes accessed | tf_op | source)
XLA Modules:
  0.0 1849.4 jit_solution(17916723392760642731)
XLA Ops:
  7.2 0.0 all-gather.2.cloned.1.call-start
  7.2 8.5 copy.21
  15.7 0.0 copy-start.14
  15.7 0.0 copy-start.12
  15.7 0.0 copy-start.15
  15.7 0.0 copy-start.1
  15.7 0.0 all-gather.2.cloned.1.call-update
  15.8 0.0 reduce-scatter.4.cloned.1.call-start
  15.8 0.6 copy-done.14
  16.4 0.2 dynamic-update-slice.1
  16.6 0.0 copy-done.12
  16.6 0.6 convert_reduce_fusion.1
  17.2 0.0 copy-done.15
  17.2 0.2 dynamic-update-slice
  17.4 35.5 %all-reduce.6 = (f32[]{:T(128)}, f32[960]{0:T(1024)S(1)}, f32[960]{0:T(1024)S(1)}) all-reduce(f32[]{:T(128)} %convert_reduce_fusion.1, f32[960]{0:T(1024)S(1)} %dynamic-update-slice.1, f32[960]{0:T(1024)S(1)} %dynamic-update-slice), channel_id=1, replica_groups=mesh['fsdp'=16] {'fsdp'}, use_global_device_ids=true, to_apply=%region_1.0 | all-reduce | flops 1921 | bytes 15368 | tf_op jit(solution)/shard_map/psum | solution.py:26
  52.9 0.0 copy-done.1
  52.9 2.4 bitcast_convert_fusion
  55.3 0.0 copy-start.10
  55.3 5.4 copy.23
  60.6 0.0 copy-done
  60.7 0.3 convert_reduce_fusion
  61.0 0.0 copy-done.10
  61.0 0.6 compare_select_fusion
  61.6 0.6 fusion.10
  62.2 0.6 copy-done.4
  62.8 0.0 copy-start.2
  62.8 1.3 convert_divide_fusion
  64.0 306.9 %all-gather.2.cloned.1.call-done = bf16[49152,960]{1,0:T(8,128)(2,1)} async-done(((bf16[3072,960]{1,0:T(8,128)(2,1)}), bf16[49152,960]{1,0:T(8,128)(2,1)}) %all-gather.2.cloned.1.call-update) | async-done | bytes 94371856 | tf_op jit(solution)/shard_map/all_gather | solution.py:23
  370.9 124.6 %fusion.20 = (f32[1024]{0:T(1024)S(1)}, f32[1024,49152]{1,0:T(8,128)}) fusion(bf16[49152,960]{1,0:T(8,128)(2,1)} %all-gather.2.cloned.1.call-done, bf16[1,1024,960]{1,2,0:T(8,128)(2,1)S(1)} %copy-done, f32[960]{0:T(1024)S(1)} %get-tuple-element.34, f32[960]{0:T(1024)S(1)} %get-tuple-element.35, f32[1024]{0:T(1024)S(1)} %fusion.14, ...), kind=kOutput, calls=%fused_computation.43 | convolution fusion | flops 96692994048 | bytes 297684480 | tf_op jit(solution)/shard_map/dot_general | solution.py:34
  495.5 0.0 copy-done.8
  495.5 0.0 copy-start.7
  495.5 70.6 %select_reduce_fusion = (f32[1024]{0:T(1024)S(1)}, f32[1024]{0:T(1024)S(1)}) fusion(f32[1024,49152]{1,0:T(8,128)} %get-tuple-element.39, s32[1024]{0:T(1024)S(1)} %bitcast.63, f32[1024]{0:T(1024)S(1)} %is-finite_select_fusion), kind=kLoop, calls=%fused_computation.3 | loop fusion | flops 251656192 | bytes 201342976 | tf_op jit(solution)/shard_map/reduce_sum | solution.py:37
  566.1 0.0 copy-done.7
  566.1 0.6 multiply_reduce_fusion
  566.8 95.8 %multiply_convert_fusion = bf16[1024,49152]{1,0:T(8,128)(2,1)} fusion(f32[1024,49152]{1,0:T(8,128)} %get-tuple-element.39, f32[1024]{0:T(1024)S(1)} %get-tuple-element.37, f32[1024]{0:T(1024)S(1)} %bitcast.62, s32[1024]{0:T(1024)S(1)} %bitcast.64), kind=kLoop, calls=%fused_computation.2 | loop fusion | flops 301989888 | bytes 302002176 | tf_op jit(solution)/shard_map/convert_element_type | solution.py:40
  662.6 0.0 copy-done.2
  662.6 0.0 copy-start.6
  662.6 121.1 %fusion.15 = f32[49152,960]{1,0:T(8,128)} fusion(bf16[1024,49152]{1,0:T(8,128)(2,1)} %multiply_convert_fusion, bf16[1,1024,960]{1,2,0:T(8,128)(2,1)S(1)} %copy-done, f32[960]{0:T(1024)S(1)} %get-tuple-element.34, f32[960]{0:T(1024)S(1)} %get-tuple-element.35, f32[1024]{0:T(1024)S(1)} %fusion.14, f32[1024]{0:T(1024)S(1)} %broadcast_multiply_fusion), kind=kOutput, calls=%fused_computation.40 | convolution fusion | flops 96642662400 | bytes 291388928 | tf_op jit(solution)/shard_map/dot_general | solution.py:43
  783.7 0.0 copy-done.6
  783.7 147.1 %scatter_fusion = f32[49152,960]{1,0:T(8,128)} fusion(f32[49152,960]{1,0:T(8,128)} %fusion.15, s32[1024]{0:T(1024)S(1)} %bitcast.59, f32[1024,960]{1,0:T(8,128)} %copy.23), kind=kCustom, calls=%fused_computation.1 | custom fusion | flops 983040 | bytes 11800576 | tf_op jit(solution)/shard_map/scatter-add | solution.py:44
  930.8 0.0 copy-start.11
  930.9 0.0 reduce-scatter.4.cloned.1.call-update
  930.9 0.7 copy-done.11
  931.5 0.6 compare_and_fusion
  932.1 0.6 broadcast_clamp_fusion
  932.7 0.0 copy-start.5
  932.7 0.0 copy-start.3
  932.7 109.1 %fusion.19 = (f32[960]{0:T(1024)S(1)}, f32[1024]{0:T(1024)S(1)}, f32[1024,960]{0,1:T(8,128)}) fusion(f32[960]{0:T(1024)S(1)} %get-tuple-element.35, f32[1024]{0:T(1024)S(1)} %broadcast_multiply_fusion, bf16[1,1024,960]{1,2,0:T(8,128)(2,1)S(1)} %copy-done, bf16[1024,49152]{1,0:T(8,128)(2,1)} %multiply_convert_fusion, ...), kind=kOutput, calls=%fused_computation.42 | convolution fusion | flops 96642662400 | bytes 200949248 | tf_op jit(solution)/shard_map/dot_general | solution.py:41
  1041.8 0.0 copy-start.9
  1041.8 0.0 copy-done.5
  1041.8 0.0 copy-done.3
  1041.8 3.7 fusion.9
  1045.5 32.7 %all-reduce.5 = (f32[]{:T(128)}, f32[960]{0:T(1024)S(1)}, f32[960]{0:T(1024)S(1)}) all-reduce(f32[]{:T(128)} %get-tuple-element.36, f32[960]{0:T(1024)S(1)} %get-tuple-element.26, f32[960]{0:T(1024)S(1)} %get-tuple-element.28), channel_id=1, replica_groups=mesh['fsdp'=16] {'fsdp'}, use_global_device_ids=true, to_apply=%region_8.9 | all-reduce | flops 1921 | bytes 15368 | tf_op jit(solution)/shard_map/psum | solution.py:38
  1078.2 0.0 copy-done.9
  1078.2 0.0 copy-start.13
  1078.2 19.2 %gather_fusion = bf16[1024,960]{1,0:T(8,128)(2,1)} fusion(bf16[49152,960]{1,0:T(8,128)(2,1)} %all-gather.2.cloned.1.call-done, s32[1024]{0:T(1024)S(1)} %copy-done.9), kind=kCustom, calls=%fused_computation | custom fusion | bytes 3936256 | tf_op jit(solution)/shard_map/jit(_take)/gather | solution.py:31
  1097.4 0.0 copy-done.13
  1097.4 3.2 bitcast_select_fusion
  1100.6 3.9 copy.24
  1104.5 0.6 dynamic-slice.1
  1105.1 0.6 dynamic-slice.2
  1105.7 4.5 fusion.12
  1110.2 719.7 %reduce-scatter.4.cloned.1.call-done = f32[3072,960]{1,0:T(8,128)} async-done(((f32[49152,960]{1,0:T(8,128)}), f32[3072,960]{1,0:T(8,128)}) %reduce-scatter.4.cloned.1.call-update) | async-done | bytes 11796496
  1829.9 12.3 copy.25
  (10 shorter events, 0.0 us)
Async XLA Ops:
  7.2 363.7 %all-gather.2.cloned.1.call-start = ((), (), s32[]{:S(2)}) async-start(), calls=%async_computation.1 | async-start | bytes 106954752 | tf_op jit(solution)/shard_map/all_gather | solution.py:23
  15.7 0.7 copy-start.14
  15.7 0.8 copy-start.12
  15.7 1.4 copy-start.15
  15.7 37.2 %copy-start.1 = (bf16[1,1024,960]{1,2,0:T(8,128)(2,1)S(1)}, bf16[1,1024,960]{1,2,0:T(8,128)(2,1)}, u32[]{:S(2)}) copy-start(bf16[1,1024,960]{1,2,0:T(8,128)(2,1)} %param.12) | copy-start | bytes 5898244
  15.8 1814.1 %reduce-scatter.4.cloned.1.call-start = ((), (), s32[]{:S(2)}) async-start(), calls=%async_computation.2 | async-start | bytes 213909504
  55.3 5.4 copy-start
  55.3 5.7 copy-start.10
  62.2 0.6 copy-start.4
  62.8 599.8 %copy-start.2 = (f32[1024]{0:T(1024)}, f32[1024]{0:T(1024)S(1)}, u32[]{:S(2)}) copy-start(f32[1024]{0:T(1024)S(1)} %fusion.14) | copy-start | bytes 12292
  370.9 124.6 %copy-start.8 = (s32[1,1024]{1,0:T(1,128)S(1)}, s32[1,1024]{1,0:T(1,128)}, u32[]{:S(2)}) copy-start(s32[1,1024]{1,0:T(1,128)} %param.9) | copy-start | bytes 12292
  495.5 70.6 %copy-start.7 = (f32[1,1024]{1,0:T(1,128)S(1)}, f32[1,1024]{1,0:T(1,128)}, u32[]{:S(2)}) copy-start(f32[1,1024]{1,0:T(1,128)} %convert_divide_fusion) | copy-start | bytes 12292
  662.6 121.2 %copy-start.6 = (s32[1024,1]{0,1:T(1,128)S(1)}, s32[1024,1]{0,1:T(1,128)}, u32[]{:S(2)}) copy-start(s32[1024,1]{0,1:T(1,128)} %compare_select_fusion) | copy-start | bytes 12292
  930.8 0.7 copy-start.11
  932.7 109.1 %copy-start.5 = (f32[1024]{0:T(1024)S(1)}, f32[1024]{0:T(1024)}, u32[]{:S(2)}) copy-start(f32[1024]{0:T(1024)} %copy-done.4) | copy-start | bytes 12292
  932.7 109.1 %copy-start.3 = (f32[1024]{0:T(1024)S(1)}, f32[1024]{0:T(1024)}, u32[]{:S(2)}) copy-start(f32[1024]{0:T(1024)} %copy-done.2) | copy-start | bytes 12292
  1041.8 36.4 %copy-start.9 = (s32[1024]{0:T(1024)S(1)}, s32[1024]{0:T(1024)}, u32[]{:S(2)}) copy-start(s32[1024]{0:T(1024)} %broadcast_clamp_fusion) | copy-start | bytes 12292
  1078.2 19.2 %copy-start.13 = (pred[1024]{0:T(1024)(128)(4,1)S(1)}, pred[1024]{0:T(1024)(128)(4,1)}, u32[]{:S(2)}) copy-start(pred[1024]{0:T(1024)(128)(4,1)} %compare_and_fusion) | copy-start | bytes 3076
Sparse Core Ops, SparseCore 0:
  15.9 354.9 all-gather.1
  931.0 898.8 reduce-scatter.3
where the time goes:
time: 1860 us; the launch traced here: 1850 us
  waiting for transfers between devices  1030 us (55%)
  matrix products  355 us (19%)
  other arithmetic  332 us (18%)
  blocking collectives  68.2 us (4%)
  local copies, waits for them, and re-layouts  52.6 us (3%)
    unnamed x3, waiting for transfers between devices  720 us
    all_gather x1, waiting for transfers between devices, device_step(): embed_table = lax.all_gather(table_shard, 'fsdp', axis=0, tiled=True)  307 us
    scatter-add x1, other arithmetic, device_step(): d_table.at[tok_flat].add(d_emb.reshape(-1, model_dim).astype(jnp.float32))  147 us
    dot_general x1, matrix products, device_step(): lax.dot_general(normed_bf, embed_table, (((1,), (1,)), ((), ())), preferr...  125 us
    dot_general x1, matrix products, device_step(): lax.dot_general(d_logits, normed_bf, (((0,), (0,)), ((), ())), preferred_...  121 us
    dot_general x1, matrix products, device_step(): jnp.dot(d_logits, embed_table, preferred_element_type=jnp.float32)  109 us
    convert_element_type x1, other arithmetic, device_step(): (weight[:, None] * (soft_probs - label_hit.astype(jnp.float32))).astype(j...  95.8 us
    reduce_sum x1, other arithmetic, device_step(): label_logit = jnp.sum(jnp.where(label_hit, logits, 0.0), axis=1)  70.6 us
  transfers between devices with their start and end apart: 2, of which 2 were waited for; matrix products, arithmetic and copies ran while one was open for 9% of the time, Pallas kernels for 0%

commit v1 on v0

v1 whole, which is shorter than its diff:
```python
import functools

import jax
import jax.numpy as jnp
from jax import lax
from jax.experimental import pallas as pl
from jax.experimental.pallas import tpu as pltpu
from jax.sharding import PartitionSpec as P

LN_EPSILON = 1e-5
F32 = jnp.float32
BF16 = jnp.bfloat16
VMEM_LIMIT = 60 * 1024 * 1024
CHUNKS = 4


def layer_norm(inputs, ln_gain, ln_bias):
    row_mean = jnp.mean(inputs, axis=-1, keepdims=True)
    centred = inputs - row_mean
    row_var = jnp.mean(centred * centred, axis=-1, keepdims=True)
    return centred * lax.rsqrt(row_var + LN_EPSILON) * ln_gain + ln_bias


def logits_body(*refs, sub, n_sub):
    e_ref, z_ref = refs[:2]
    lt_ref, zo_ref, m_ref, s_ref = refs[-4:]
    z = z_ref[...]
    zo_ref[...] = z
    m = s = None
    for j in range(n_sub):
        rows = slice(j * sub, (j + 1) * sub)
        l = lax.dot_general(e_ref[rows, :], z, (((1,), (1,)), ((), ())), preferred_element_type=F32)
        lt_ref[rows, :] = l
        m_here = jnp.max(l, axis=0, keepdims=True)
        if m is None:
            m_new = m_here
            s = jnp.sum(jnp.exp(l - m_new), axis=0, keepdims=True)
        else:
            m_new = jnp.maximum(m, m_here)
            s = s * jnp.exp(m - m_new) + jnp.sum(jnp.exp(l - m_new), axis=0, keepdims=True)
        m = m_new
    m_ref[...] = m
    s_ref[...] = s


def logits_pass(e, z, carry, chunk, total, pt=512, sub=256):
    n_v, dim = e.shape
    n_p = z.shape[0]
    steps = n_p // pt
    first = chunk * steps
    in_specs = [pl.BlockSpec((n_v, dim), lambda i: (0, 0), pipeline_mode=pl.Buffered(1)), pl.BlockSpec((pt, dim), lambda i: (i, 0))]
    operands = [e, z]
    aliases = {}
    if carry is not None:
        in_specs += [pl.BlockSpec(memory_space=pl.ANY)] * 2
        operands += list(carry)
        aliases = {2: 0, 3: 1}
    return pl.pallas_call(
        functools.partial(logits_body, sub=sub, n_sub=n_v // sub),
        grid=(steps,),
        in_specs=in_specs,
        out_specs=[
            pl.BlockSpec((n_v, pt), lambda i: (0, i + first)),
            pl.BlockSpec((pt, dim), lambda i: (i + first, 0)),
            pl.BlockSpec((1, pt), lambda i: (0, i)),
            pl.BlockSpec((1, pt), lambda i: (0, i)),
        ],
        out_shape=[
            jax.ShapeDtypeStruct((n_v, total), F32),
            jax.ShapeDtypeStruct((total, dim), BF16),
            jax.ShapeDtypeStruct((1, n_p), F32),
            jax.ShapeDtypeStruct((1, n_p), F32),
        ],
        input_output_aliases=aliases,
        compiler_params=pltpu.CompilerParams(vmem_limit_bytes=VMEM_LIMIT, dimension_semantics=("arbitrary",)),
        cost_estimate=pl.CostEstimate(flops=2 * n_v * n_p * dim, bytes_accessed=4 * n_v * n_p + 2 * n_v * dim, transcendentals=n_v * n_p),
        name="logits_pass",
    )(*operands)


def table_grad_body(base_ref, lt_ref, z_ref, lse_ref, w_ref, y_ref, acc_ref, ll_ref, *, sub, n_sub):
    @pl.when(pl.program_id(0) == 0)
    def _():
        acc_ref[...] = jnp.zeros_like(acc_ref)

    lse = lse_ref[...]
    w = w_ref[...]
    y = y_ref[...] - base_ref[0]
    z = z_ref[...]
    row_ids = lax.broadcasted_iota(jnp.int32, (sub, z.shape[0]), 0)
    label_logit = jnp.zeros_like(lse)
    for j in range(n_sub):
        rows = slice(j * sub, (j + 1) * sub)
        l = lt_ref[rows, :]
        p = jnp.exp(l - lse)
        hit = row_ids == (y - j * sub)
        d = (w * jnp.where(hit, p - 1.0, p)).astype(BF16)
        label_logit = label_logit + jnp.sum(jnp.where(hit, l, 0.0), axis=0, keepdims=True)
        acc_ref[rows, :] += jnp.dot(d, z, preferred_element_type=F32)
    ll_ref[...] = label_logit


def table_grad(base, lt, z, lse, w, y, pt=1024, sub=256):
    n_v, n_p = lt.shape
    dim = z.shape[1]
    row = pl.BlockSpec((1, pt), lambda i, b: (0, i))
    return pl.pallas_call(
        functools.partial(table_grad_body, sub=sub, n_sub=n_v // sub),
        grid_spec=pltpu.PrefetchScalarGridSpec(
            num_scalar_prefetch=1,
            grid=(n_p // pt,),
            in_specs=[pl.BlockSpec((n_v, pt), lambda i, b: (0, i)), pl.BlockSpec((pt, dim), lambda i, b: (i, 0)), row, row, row],
            out_specs=[pl.BlockSpec((n_v, dim), lambda i, b: (0, 0), pipeline_mode=pl.Buffered(1)), row],
        ),
        out_shape=[jax.ShapeDtypeStruct((n_v, dim), F32), jax.ShapeDtypeStruct((1, n_p), F32)],
        compiler_params=pltpu.CompilerParams(vmem_limit_bytes=VMEM_LIMIT, dimension_semantics=("arbitrary",)),
        cost_estimate=pl.CostEstimate(flops=2 * n_v * n_p * dim, bytes_accessed=4 * n_v * n_p, transcendentals=n_v * n_p),
        name="table_grad",
    )(base, lt, z, lse, w, y)


def hidden_grad_body(base_ref, z_ref, e_ref, lse_ref, w_ref, y_ref, acc_ref, *, tp, n_tp, tv):
    i = pl.program_id(0)

    @pl.when(i == 0)
    def _():
        acc_ref[...] = jnp.zeros_like(acc_ref)

    e = e_ref[...]
    base = base_ref[0] + i * tv
    col_ids = lax.broadcasted_iota(jnp.int32, (tp, tv), 1)
    for j in range(n_tp):
        rows = slice(j * tp, (j + 1) * tp)
        l = lax.dot_general(z_ref[rows, :], e, (((1,), (1,)), ((), ())), preferred_element_type=F32)
        p = jnp.exp(l - lse_ref[rows, :])
        hit = col_ids == (y_ref[rows, :] - base)
        d = (w_ref[rows, :] * jnp.where(hit, p - 1.0, p)).astype(BF16)
        acc_ref[rows, :e.shape[1]] += jnp.dot(d, e, preferred_element_type=F32)


def hidden_grad(base, z, e, lse, w, y, tp=512, tv=768):
    n_v, dim = e.shape
    n_p = z.shape[0]
    wide = pl.cdiv(dim, 128) * 128
    col = pl.BlockSpec((n_p, 1), lambda i, b: (0, 0))
    return pl.pallas_call(
        functools.partial(hidden_grad_body, tp=tp, n_tp=n_p // tp, tv=tv),
        grid_spec=pltpu.PrefetchScalarGridSpec(
            num_scalar_prefetch=1,
            grid=(n_v // tv,),
            in_specs=[pl.BlockSpec((n_p, dim), lambda i, b: (0, 0)), pl.BlockSpec((tv, dim), lambda i, b: (i, 0)), col, col, col],
            out_specs=pl.BlockSpec((n_p, wide), lambda i, b: (0, 0), pipeline_mode=pl.Buffered(1)),
        ),
        out_shape=jax.ShapeDtypeStruct((n_p, wide), F32),
        compiler_params=pltpu.CompilerParams(vmem_limit_bytes=VMEM_LIMIT, dimension_semantics=("arbitrary",)),
        cost_estimate=pl.CostEstimate(flops=4 * n_v * n_p * dim, bytes_accessed=2 * n_v * dim, transcendentals=n_v * n_p),
        name="hidden_grad",
    )(base, z, e, lse, w, y)


def add_rows_body(count_ref, code_ref, de_ref, grad_ref, acc_ref, rows_ref):
    b = pl.program_id(0)

    @pl.when(b == 0)
    def _():
        acc_ref[...] = grad_ref[...]

    rows_ref[...] = de_ref[...].astype(F32)

    def step(k, carry):
        code = code_ref[0, 0, k]
        src = lax.shift_right_logical(code, 12)
        dst = lax.bitwise_and(code, 4095)
        acc_ref[pl.ds(dst, 1), :] += rows_ref[pl.ds(src, 1), :]
        return carry

    lax.fori_loop(0, count_ref[b], step, 0)


def add_rows(counts, codes, d_emb, grad):
    n_b, n_p = codes.shape
    n_v, dim = grad.shape
    whole = lambda b, c: (0, 0)
    return pl.pallas_call(
        add_rows_body,
        grid_spec=pltpu.PrefetchScalarGridSpec(
            num_scalar_prefetch=1,
            grid=(n_b,),
            in_specs=[
                pl.BlockSpec((1, 1, n_p), lambda b, c: (b, 0, 0), memory_space=pltpu.SMEM),
                pl.BlockSpec((n_p, dim), lambda b, c: (b, 0)),
                pl.BlockSpec((n_v, dim), whole, pipeline_mode=pl.Buffered(1)),
            ],
            out_specs=pl.BlockSpec((n_v, dim), whole, pipeline_mode=pl.Buffered(1)),
            scratch_shapes=[pltpu.VMEM((n_p, dim), F32)],
        ),
        out_shape=jax.ShapeDtypeStruct((n_v, dim), F32),
        compiler_params=pltpu.CompilerParams(vmem_limit_bytes=VMEM_LIMIT, dimension_semantics=("arbitrary",)),
        cost_estimate=pl.CostEstimate(flops=10**10, bytes_accessed=2 * n_b * n_p * dim, transcendentals=0),
        name="add_rows",
    )(counts, codes.reshape(n_b, 1, n_p), d_emb, grad)


def exchange_body(x_ref, out_ref, send_sem, recv_sem, *, axis, n_dev, split):
    me = lax.axis_index(axis)
    barrier = pltpu.get_barrier_semaphore()
    for k in range(1, n_dev):
        pl.semaphore_signal(barrier, inc=1, device_id=(lax.rem(me + k, n_dev),), device_id_type=pl.DeviceIdType.MESH)
    pl.semaphore_wait(barrier, n_dev - 1)
    copies = []
    for k in range(1, n_dev):
        to = lax.rem(me + k, n_dev)
        copy = pltpu.make_async_remote_copy(
            src_ref=x_ref.at[to] if split else x_ref.at[0],
            dst_ref=out_ref.at[me],
            send_sem=send_sem.at[k - 1],
            recv_sem=recv_sem.at[k - 1],
            device_id=(to,),
            device_id_type=pl.DeviceIdType.MESH,
        )
        copy.start()
        copies.append(copy)
    out_ref[pl.ds(me, 1)] = x_ref[pl.ds(me, 1)] if split else x_ref[...]
    for copy in copies:
        copy.wait()


def exchange(x, n_dev, split, collective_id, axis='fsdp'):
    block = x.shape[1:]
    return pl.pallas_call(
        functools.partial(exchange_body, axis=axis, n_dev=n_dev, split=split),
        in_specs=[pl.BlockSpec(memory_space=pltpu.VMEM)],
        out_specs=pl.BlockSpec(memory_space=pltpu.VMEM),
        out_shape=jax.ShapeDtypeStruct((n_dev,) + block, x.dtype),
        scratch_shapes=[pltpu.SemaphoreType.DMA((n_dev - 1,)), pltpu.SemaphoreType.DMA((n_dev - 1,))],
        compiler_params=pltpu.CompilerParams(collective_id=collective_id, has_side_effects=True),
        cost_estimate=pl.CostEstimate(flops=4 * 10**9, bytes_accessed=0, transcendentals=0),
        name="exchange",
    )(x)


def solution(mesh):
    batch_spec = P('fsdp', None)
    act_spec = P('fsdp', None, None)
    vec_spec = P('fsdp')
    n_dev = mesh.shape['fsdp']
    half = n_dev // 2
    planes = [list(range(half)), list(range(half, n_dev))]
    partner = [(i, (i + half) % n_dev) for i in range(n_dev)]

    def device_step(tokens, labels, loss_mask, hidden, d_emb, table_shard, gain_shard, bias_shard):
        _, seq, dim = hidden.shape
        n_v = table_shard.shape[0]
        feat = gain_shard.shape[0]
        total = n_dev * seq
        part = seq // CHUNKS
        me = lax.axis_index('fsdp')
        other = lax.rem(me + half, n_dev)
        plane = me // half

        small = jnp.concatenate([tokens.reshape(-1).astype(F32), labels.reshape(-1).astype(F32), loss_mask.reshape(-1).astype(F32), gain_shard, bias_shard])
        small = jnp.pad(small, (0, 4 * 1024 - small.shape[0])).reshape(1, 32, 128)
        small = exchange(small, n_dev, False, 1).reshape(n_dev, 4 * 1024)
        tok_all = small[:, :seq].astype(jnp.int32)
        label_all = small[:, seq:2 * seq].astype(jnp.int32)
        mask_all = small[:, 2 * seq:3 * seq]
        ln_gain = small[:, 3 * seq:3 * seq + feat].reshape(-1)
        ln_bias = small[:, 3 * seq + feat:3 * seq + 2 * feat].reshape(-1)
        weight_all = mask_all / jnp.sum(mask_all)

        hid = hidden.reshape(seq, dim).astype(F32)
        normed, ln_vjp = jax.vjp(layer_norm, hid, ln_gain, ln_bias)
        z = normed.astype(BF16)

        carry = None
        maxes, sums, z_parts = [], [], []
        for c in range(CHUNKS):
            z_c = lax.all_gather(z[c * part:(c + 1) * part], 'fsdp', axis=0, tiled=True)
            lt, z_all, m_c, s_c = logits_pass(table_shard, z_c, carry, c, total)
            carry = (lt, z_all)
            maxes.append(m_c)
            sums.append(s_c)
            z_parts.append(lax.dynamic_slice_in_dim(z_c, other * part, part, 0))
        z_other = jnp.concatenate(z_parts, axis=0)

        def to_owner(parts):
            return jnp.stack([p.reshape(n_dev, part) for p in parts], axis=1).reshape(n_dev, seq // 128, 128)

        pairs = jnp.concatenate([to_owner(maxes), to_owner(sums)], axis=1)
        pairs = exchange(pairs, n_dev, True, 2)
        pair_max, pair_sum = pairs[:, :seq // 128], pairs[:, seq // 128:]
        row_max = jnp.max(pair_max, axis=0)
        row_sum = jnp.sum(pair_sum * jnp.exp(pair_max - row_max[None]), axis=0)
        lse_all = exchange((row_max + jnp.log(row_sum))[None], n_dev, False, 3).reshape(n_dev, seq)

        def by_chunk(a):
            return a.reshape(n_dev, CHUNKS, part).transpose(1, 0, 2).reshape(1, total)

        base = (me * n_v).astype(jnp.int32).reshape(1)
        w_row = by_chunk(weight_all)
        d_table, label_logit = table_grad(base, lt, z_all, by_chunk(lse_all), w_row, by_chunk(label_all))
        loss_lse = jnp.sum(weight_all * lse_all)
        loss_hit = jnp.sum(w_row * label_logit)

        e_half = lax.all_gather(table_shard, 'fsdp', axis=0, tiled=True, axis_index_groups=planes)
        half_base = (plane * half * n_v).astype(jnp.int32)

        def row_of(a, d):
            return lax.dynamic_index_in_dim(a, d, 0, keepdims=False)

        def half_grad(d, z_d):
            return hidden_grad(half_base.reshape(1), z_d, e_half, row_of(lse_all, d)[:, None], row_of(weight_all, d)[:, None], row_of(label_all, d)[:, None])

        dz_other = half_grad(other, z_other)
        dz_other = lax.ppermute(dz_other, 'fsdp', partner)
        dz_own = half_grad(me, z)

        tok_own = row_of(tok_all, me)
        in_half = (tok_own // (half * n_v)) == plane
        look = jnp.concatenate([row_of(tok_all, other), tok_own]) - half_base
        found = jnp.take(e_half, jnp.clip(look, 0, half * n_v - 1), axis=0, mode='clip')
        found_other = lax.ppermute(found[:seq], 'fsdp', partner)
        emb_rows = jnp.where(in_half[:, None], found[seq:], found_other).reshape(1, seq, dim)

        de_all = lax.all_gather(d_emb.reshape(seq, dim), 'fsdp', axis=0, tiled=True)
        rel = tok_all - me * n_v
        mine = (rel >= 0) & (rel < n_v)
        upto = (jnp.arange(seq)[:, None] <= jnp.arange(seq)[None, :]).astype(BF16)
        rank = jnp.dot(mine.astype(BF16), upto, preferred_element_type=F32).astype(jnp.int32) - 1
        code = jnp.where(mine, jnp.arange(seq, dtype=jnp.int32)[None, :] * 4096 + rel, 0)
        slot = jnp.where(mine, rank, -1)
        codes = jnp.sum(jnp.where(slot[:, :, None] == jnp.arange(seq, dtype=jnp.int32)[None, None, :], code[:, :, None], 0), axis=1)
        counts = jnp.sum(mine.astype(jnp.int32), axis=1)
        d_table, dz_own = lax.optimization_barrier((d_table, dz_own))
        d_table = add_rows(counts, codes, de_all, d_table)

        d_hidden, d_gain, d_bias = ln_vjp((dz_own + dz_other)[:, :dim])
        tail = jnp.concatenate([d_gain.reshape(n_dev, feat), d_bias.reshape(n_dev, feat), jnp.broadcast_to(loss_hit, (n_dev, 8))], axis=1)
        tail = jnp.sum(exchange(tail[:, None, :], n_dev, True, 4), axis=0)[0]
        mean_loss = loss_lse - tail[2 * feat]
        return (emb_rows, mean_loss, d_hidden.astype(BF16).reshape(1, seq, dim), d_table, tail[:feat], tail[feat:2 * feat])

    return jax.shard_map(device_step, mesh=mesh, in_specs=(batch_spec, batch_spec, batch_spec, act_spec, act_spec, batch_spec, vec_spec, vec_spec), out_specs=(act_spec, P(), act_spec, batch_spec, vec_spec, vec_spec), check_vma=False)
```

time: 1860 us -> 889 us (0.48)
  waiting for transfers between devices: 1030 us -> 69 us
  Pallas kernels: 0 us -> 612 us
  matrix products: 355 us -> 0.34 us
  other arithmetic: 332 us -> 37.5 us
  blocking collectives: 68.2 us -> 0 us
  local copies, waits for them, and re-layouts: 52.6 us -> 116 us
  starting transfers between devices: 0.08 us -> 31.3 us
    unnamed x3 -> x6, waiting for transfers between devices: 720 us -> 1.95 us
    pallas_call x0 -> x12, Pallas kernels: none -> 612 us  [the longest x2 242 us: hidden_grad(): pl.pallas_call(functools.partial(hidden_grad_body, tp=tp, n_tp=n_p // tp,...]
    dot_general x3 -> x1, matrix products: 355 us -> 0.34 us  [device_step(): jnp.dot(mine.astype(BF16), upto, preferred_element_type=F32)]
    all_gather x1 -> x6, waiting for transfers between devices: 307 us -> 67 us  [the longest x4 51.5 us: device_step(): z_c = lax.all_gather(z[c * part:(c + 1) * part], 'fsdp', axis=0, tiled=True)]
    scatter-add x1 -> x0, other arithmetic: 147 us -> none  [device_step(): d_table.at[tok_flat].add(d_emb.reshape(-1, model_dim).astype(jnp.float32))]
    convert_element_type x2 -> x4, other arithmetic: 98.2 us -> 0.84 us  [the longest x1 0.82 us: device_step(): z = normed.astype(BF16)]
    psum x2 -> x0, blocking collectives: 68.2 us -> none  [the longest x1 35.5 us: device_step(): mask_count = lax.psum(jnp.sum(loss_mask.astype(jnp.float32)), 'fsdp')]
    reduce_sum x3 -> x8, other arithmetic: 71.8 us -> 18.8 us  [the longest x1 8.79 us: device_step(): jnp.sum(jnp.where(slot[:, :, None] == jnp.arange(seq, dtype=jnp.int32)[No...]
  transfers between devices with their start and end apart: 2 -> 8, of which waited for: 2 -> 5; matrix products, arithmetic and copies ran while one was open for 9% -> 14% of each run, Pallas kernels for 0% -> 67%
where the time goes in v1:
time: 889 us; the launch traced here: 883 us
  Pallas kernels  612 us (69%)
  local copies, waits for them, and re-layouts  116 us (13%)
  waiting for transfers between devices  69 us (8%)
  other arithmetic  37.5 us (4%)
  starting transfers between devices  31.3 us (4%)
  between operations  17.3 us (2%)
    pallas_call x2, Pallas kernels, hidden_grad(): pl.pallas_call(functools.partial(hidden_grad_body, tp=tp, n_tp=n_p // tp,...  242 us
    pallas_call x4, Pallas kernels, logits_pass(): pl.pallas_call(functools.partial(logits_body, sub=sub, n_sub=n_v // sub),...  168 us
    pallas_call x1, Pallas kernels, table_grad(): pl.pallas_call(functools.partial(table_grad_body, sub=sub, n_sub=n_v // s...  132 us
    gather x1, local copies, waits for them, and re-layouts, device_step(): jnp.take(e_half, jnp.clip(look, 0, half * n_v - 1), axis=0, mode='clip')  53.5 us
    all_gather x4, waiting for transfers between devices, device_step(): z_c = lax.all_gather(z[c * part:(c + 1) * part], 'fsdp', axis=0, tiled=True)  51.5 us
    unnamed x64, local copies, waits for them, and re-layouts  36.8 us
    pallas_call x1, Pallas kernels, add_rows(): pl.pallas_call(add_rows_body, grid_spec=pltpu.PrefetchScalarGridSpec(num_...  35.7 us
    pallas_call x4, Pallas kernels, exchange(): pl.pallas_call(functools.partial(exchange_body, axis=axis, n_dev=n_dev, s...  35.4 us
  transfers between devices with their start and end apart: 8, of which 5 were waited for; matrix products, arithmetic and copies ran while one was open for 14% of the time, Pallas kernels for 67%

profile of v1, /device:TPU:0, one launch (start us, length us, event | category | flops | bytes accessed | tf_op | source)
XLA Modules:
  0.0 883.5 jit_solution(16964745648771977432)
XLA Ops:
  7.3 2.8 copy.100
  10.5 0.7 fusion.10
  12.0 11.3 %exchange.4 = f32[16,32,128]{2,1,0:T(8,128)} custom-call(f32[1,32,128]{2,1,0:T(8,128)} %pad_bitcast_fusion.x_ref), custom_call_target="tpu_custom_call" | custom-call | flops 4000000000 | tf_op jit(solution)/shard_map/exchange/pallas_call | solution.py:230
  23.4 1.1 copy.137
  24.8 0.8 fusion.8.z_ref
  25.6 1.3 copy-done.2
  26.9 1.4 fusion.23
  28.4 0.7 all-gather.12.cloned.1.call-update
  30.4 8.5 copy.97.refs_0_
  39.5 1.0 copy-done.3
  40.5 2.5 copy.122
  43.5 8.8 select_reduce_fusion
  52.9 0.7 convert_reduce_fusion.1.count_ref
  54.2 23.8 %all-gather.10.cloned.1.call-done.refs_1_ = bf16[4096,960]{1,0:T(8,128)(2,1)} async-done(((bf16[256,960]{1,0:T(8,128)(2,1)}), bf16[4096,960]{1,0:T(8,128)(2,1)}) %all-gather.10.cloned.1.call-update) | async-done | bytes 7864336 | tf_op jit(solution)/shard_map/all_gather | solution.py:278
  78.1 41.9 %logits_pass.4 = (f32[3072,16384]{1,0:T(8,128)}, bf16[16384,960]{1,0:T(8,128)(2,1)}, f32[1,4096]{1,0:T(1,128)}, f32[1,4096]{1,0:T(1,128)}) custom-call(bf16[3072,960]{1,0:T(8,128)(2,1)} %copy.97.refs_0_, bf16[4096,960]{1,0:T(8,128)(2,1)} %all-gather.10.cloned.1.call-done.refs_1_), custom_call_target="tpu_custom_call" | custom-call | flops 24159191040 | bytes 56229888 | tf_op jit(solution)/shard_map/logits_pass/pallas_call | solution.py:58
  119.9 9.1 %all-gather.12.cloned.1.call-done.refs_1_ = bf16[4096,960]{1,0:T(8,128)(2,1)} async-done(((bf16[256,960]{1,0:T(8,128)(2,1)}), bf16[4096,960]{1,0:T(8,128)(2,1)}) %all-gather.12.cloned.1.call-update) | async-done | bytes 7864336 | tf_op jit(solution)/shard_map/all_gather | solution.py:278
  129.0 41.8 %logits_pass.5 = (f32[3072,16384]{1,0:T(8,128)}, bf16[16384,960]{1,0:T(8,128)(2,1)}, f32[1,4096]{1,0:T(1,128)}, f32[1,4096]{1,0:T(1,128)}) custom-call(bf16[3072,960]{1,0:T(8,128)(2,1)} %copy.97.refs_0_, bf16[4096,960]{1,0:T(8,128)(2,1)} %all-gather.12.cloned.1.call-done.refs_1_, ...), custom_call_target="tpu_custom_call", output_to_operand_aliasing={{0}: (2, {}), {1}: (3, {})} | custom-call | flops 24159191040 | bytes 56229888 | tf_op jit(solution)/shard_map/logits_pass/pallas_call | solution.py:58
  170.8 9.1 %all-gather.14.cloned.1.call-done.refs_1_ = bf16[4096,960]{1,0:T(8,128)(2,1)} async-done(((bf16[256,960]{1,0:T(8,128)(2,1)}), bf16[4096,960]{1,0:T(8,128)(2,1)}) %all-gather.14.cloned.1.call-update) | async-done | bytes 7864336 | tf_op jit(solution)/shard_map/all_gather | solution.py:278
  179.9 41.9 %logits_pass.6 = (f32[3072,16384]{1,0:T(8,128)}, bf16[16384,960]{1,0:T(8,128)(2,1)}, f32[1,4096]{1,0:T(1,128)}, f32[1,4096]{1,0:T(1,128)}) custom-call(bf16[3072,960]{1,0:T(8,128)(2,1)} %copy.97.refs_0_, bf16[4096,960]{1,0:T(8,128)(2,1)} %all-gather.14.cloned.1.call-done.refs_1_, ...), custom_call_target="tpu_custom_call", output_to_operand_aliasing={{0}: (2, {}), {1}: (3, {})} | custom-call | flops 24159191040 | bytes 56229888 | tf_op jit(solution)/shard_map/logits_pass/pallas_call | solution.py:58
  221.9 9.4 %all-gather.16.cloned.1.call-done.refs_1_ = bf16[4096,960]{1,0:T(8,128)(2,1)} async-done(((bf16[256,960]{1,0:T(8,128)(2,1)}), bf16[4096,960]{1,0:T(8,128)(2,1)}) %all-gather.16.cloned.1.call-update) | async-done | bytes 7864336 | tf_op jit(solution)/shard_map/all_gather | solution.py:278
  231.3 42.0 %logits_pass.7 = (f32[3072,16384]{1,0:T(8,128)}, bf16[16384,960]{1,0:T(8,128)(2,1)}, f32[1,4096]{1,0:T(1,128)}, f32[1,4096]{1,0:T(1,128)}) custom-call(bf16[3072,960]{1,0:T(8,128)(2,1)} %copy.97.refs_0_, bf16[4096,960]{1,0:T(8,128)(2,1)} %all-gather.16.cloned.1.call-done.refs_1_, ...), custom_call_target="tpu_custom_call", output_to_operand_aliasing={{0}: (2, {}), {1}: (3, {})} | custom-call | flops 24159191040 | bytes 56229888 | tf_op jit(solution)/shard_map/logits_pass/pallas_call | solution.py:58
  273.3 0.8 pad_maximum_fusion.2
  274.2 0.8 pad_maximum_fusion.3
  275.6 9.3 %exchange.5 = f32[16,16,128]{2,1,0:T(8,128)} custom-call(f32[16,16,128]{2,1,0:T(8,128)} %pad_maximum_fusion.1.x_ref), custom_call_target="tpu_custom_call" | custom-call | flops 4000000000 | tf_op jit(solution)/shard_map/exchange/pallas_call | solution.py:230
  285.0 0.9 slice_reduce_fusion.1
  285.8 0.9 multiply_reduce_fusion.2
  287.3 7.7 exchange.6
  295.1 0.9 reshape_reshape.3
  296.0 0.9 copy.138
  296.8 2.1 multiply_reduce_fusion.1
  299.0 1.1 copy.116.lse_ref
  300.0 1.0 copy.117.w_ref
  301.1 1.0 copy.118.y_ref
  302.1 0.7 reshape.216.w_ref
  302.8 0.7 reshape.218.y_ref
  303.5 0.7 reshape.214.lse_ref
  304.2 1.0 copy.119.lse_ref
  305.2 1.0 copy.120.w_ref
  306.2 1.0 copy.121.y_ref
  307.3 131.9 %table_grad.1 = (f32[3072,960]{1,0:T(8,128)}, f32[1,16384]{1,0:T(1,128)}) custom-call(s32[1]{0:T(128)} %bitcast.19.base_ref, f32[3072,16384]{1,0:T(8,128)} %get-tuple-element.40.lt_ref, bf16[16384,960]{1,0:T(8,128)(2,1)} %get-tuple-element.41.z_ref, f32[1,16384]{1,0:T(1,128)} %reshape.214.lse_ref, f32[1,16384]{1,0:T(1,128)} %reshape.216.w_ref, ...), custom_call_target="tpu_custom_call" | custom-call | flops 96636764160 | bytes 201326592 | tf_op jit(solution)/shard_map/table_grad/pallas_call | solution.py:107
  439.2 1.6 multiply_reduce_fusion
  442.0 1.1 constant_dynamic-slice_fusion
  443.1 1.1 constant_dynamic-slice_fusion.1
  444.2 1.1 constant_dynamic-slice_fusion.2
  445.3 1.1 constant_dynamic-slice_fusion.3
  446.4 1.6 pad_maximum_fusion.z_ref
  448.6 15.5 %all-gather.8.cloned.1.call-done.e_ref = bf16[24576,960]{1,0:T(8,128)(2,1)} async-done(((bf16[3072,960]{1,0:T(8,128)(2,1)}), bf16[24576,960]{1,0:T(8,128)(2,1)}) %all-gather.8.cloned.1.call-update) | async-done | bytes 47185936 | tf_op jit(solution)/shard_map/all_gather | solution.py:305
  464.2 120.9 %hidden_grad.3 = f32[1024,1024]{1,0:T(8,128)} custom-call(s32[1]{0:T(128)} %bitcast.23.base_ref, bf16[1024,960]{1,0:T(8,128)(2,1)} %pad_maximum_fusion.z_ref, bf16[24576,960]{1,0:T(8,128)(2,1)} %all-gather.8.cloned.1.call-done.e_ref, f32[1024,1]{1,0:T(8,128)} %copy.119.lse_ref, f32[1024,1]{1,0:T(8,128)} %copy.120.w_ref, s32[1024,1]{1,0:T(8,128)} %copy.121.y_ref), custom_call_target="tpu_custom_call" | custom-call | flops 96636764160 | bytes 47185920 | tf_op jit(solution)/shard_map/hidden_grad/pallas_call | solution.py:146
  585.1 1.5 collective-permute-start.1
  586.6 53.5 %gather_fusion = bf16[2048,960]{1,0:T(8,128)(2,1)} fusion(bf16[24576,960]{1,0:T(8,128)(2,1)} %all-gather.8.cloned.1.call-done.e_ref, s32[2048]{0:T(1024)S(1)} %broadcast_clamp_fusion), kind=kCustom, calls=%fused_computation | custom fusion | bytes 7872512 | tf_op jit(solution)/shard_map/jit(_take)/gather | solution.py:321
  640.1 1.6 slice-done
  641.6 2.4 copy.98
  644.0 29.1 %collective-permute-start = (bf16[1024,960]{0,1:T(8,128)(2,1)}, bf16[1024,960]{0,1:T(8,128)(2,1)S(1)}, u32[]{:S(2)}, u32[]{:S(2)}) collective-permute-start(bf16[1024,960]{0,1:T(8,128)(2,1)} %copy.98), channel_id=1, source_target_pairs={{0,8},{1,9},{2,10},{3,11},{4,12},{5,13},{6,14},{7,15},{8,0},{9,1},... | collective-permute-start | bytes 5898248 | tf_op jit(solution)/shard_map/ppermute | solution.py:322
  673.1 120.8 %hidden_grad.2 = f32[1024,1024]{1,0:T(8,128)} custom-call(s32[1]{0:T(128)} %bitcast.23.base_ref, bf16[1024,960]{1,0:T(8,128)(2,1)} %copy-done.2, bf16[24576,960]{1,0:T(8,128)(2,1)} %all-gather.8.cloned.1.call-done.e_ref, f32[1024,1]{1,0:T(8,128)} %copy.116.lse_ref, f32[1024,1]{1,0:T(8,128)} %copy.117.w_ref, s32[1024,1]{1,0:T(8,128)} %copy.118.y_ref), custom_call_target="tpu_custom_call" | custom-call | flops 96636764160 | bytes 47185920 | tf_op jit(solution)/shard_map/hidden_grad/pallas_call | solution.py:146
  793.9 35.7 %add_rows.1 = f32[3072,960]{1,0:T(8,128)} custom-call(s32[16]{0:T(128)} %convert_reduce_fusion.1.count_ref, s32[16,1,1024]{2,1,0:T(1,128)} %reshape.223.code_ref, bf16[16384,960]{1,0:T(8,128)(2,1)} %bitcast.104, f32[3072,960]{1,0:T(8,128)} %get-tuple-element.45.grad_ref), custom_call_target="tpu_custom_call" | custom-call | flops 10000000000 | bytes 31457280 | tf_op jit(solution)/shard_map/add_rows/pallas_call | solution.py:184
  829.6 12.3 %copy.125 = f32[3072,960]{0,1:T(8,128)} copy(f32[3072,960]{1,0:T(8,128)} %add_rows.1) | data formatting | bytes 23592960
  841.8 2.5 copy.99
  844.4 4.0 fusion.14
  848.4 3.9 copy.123
  852.3 5.8 fusion.11
  859.0 7.0 exchange.7
  866.0 0.7 reduce_sum.143
  867.9 3.4 fusion.22
  871.6 2.4 copy.124
  (108 shorter events, 10.6 us)
Async XLA Ops:
  7.2 4.1 copy-start.21
  7.2 4.1 copy-start.22
  7.2 4.1 copy-start.23
  7.2 4.1 copy-start.26
  7.2 4.1 copy-start.27
  7.2 70.9 %all-gather.10.cloned.1.call-start = ((), (), s32[]{:S(2)}) async-start(), calls=%async_computation.1 | async-start | bytes 8912896 | tf_op jit(solution)/shard_map/all_gather | solution.py:278
  10.1 14.7 %copy-start = (bf16[1,1024,960]{2,1,0:T(8,128)(2,1)}, bf16[1,1024,960]{2,1,0:T(8,128)(2,1)S(1)}, u32[]{:S(2)}) copy-start(bf16[1,1024,960]{2,1,0:T(8,128)(2,1)S(1)} %copy.100) | copy-start | bytes 5898244
  10.5 14.3 %copy-start.7 = (f32[1024]{0:T(1024)}, f32[1024]{0:T(1024)S(1)}, u32[]{:S(2)}) copy-start(f32[1024]{0:T(1024)S(1)} %broadcast_multiply_fusion) | copy-start | bytes 12292
  11.2 12.2 %copy-start.13 = (f32[1024]{0:T(1024)}, f32[1024]{0:T(1024)S(1)}, u32[]{:S(2)}) copy-start(f32[1024]{0:T(1024)S(1)} %fusion.10) | copy-start | bytes 12292
  11.2 13.5 %copy-start.11 = (f32[1024]{0:T(1024)}, f32[1024]{0:T(1024)S(1)}, u32[]{:S(2)}) copy-start(f32[1024]{0:T(1024)S(1)} %fusion.20) | copy-start | bytes 12292
  24.5 29.1 %copy-start.4 = (f32[2,8,32,128]{3,1,2,0:T(8,128)}, f32[2,8,32,128]{3,1,2,0:T(8,128)S(1)}, u32[]{:S(2)}) copy-start(f32[2,8,32,128]{3,1,2,0:T(8,128)S(1)} %copy.137) | copy-start | bytes 786436
  24.7 3.7 copy-start.9
  25.6 1.3 copy-start.2
  28.3 100.7 %all-gather.12.cloned.1.call-start = ((), (), s32[]{:S(2)}) async-start(), calls=%async_computation.2 | async-start | bytes 8912896 | tf_op jit(solution)/shard_map/all_gather | solution.py:278
  29.1 150.8 %all-gather.14.cloned.1.call-start = ((), (), s32[]{:S(2)}) async-start(), calls=%async_computation.3 | async-start | bytes 8912896 | tf_op jit(solution)/shard_map/all_gather | solution.py:278
  29.8 201.5 %all-gather.16.cloned.1.call-start = ((), (), s32[]{:S(2)}) async-start(), calls=%async_computation.4 | async-start | bytes 8912896 | tf_op jit(solution)/shard_map/all_gather | solution.py:278
  30.4 433.8 %all-gather.8.cloned.1.call-start = ((), (), s32[]{:S(2)}) async-start(), calls=%async_computation | async-start | bytes 56623104 | tf_op jit(solution)/shard_map/all_gather | solution.py:305
  39.0 1.5 copy-start.3
  39.0 754.9 %all-gather.18.cloned.1.call-start = ((), (), s32[]{:S(2)}) async-start(), calls=%async_computation.5 | async-start | bytes 35651584 | tf_op jit(solution)/shard_map/all_gather | solution.py:325
  231.3 42.0 %copy-start.16 = (f32[1,4096]{1,0:T(1,128)S(1)}, f32[1,4096]{1,0:T(1,128)}, u32[]{:S(2)}) copy-start(f32[1,4096]{1,0:T(1,128)} %get-tuple-element.26) | copy-start | bytes 49156
  231.3 42.0 %copy-start.18 = (f32[1,4096]{1,0:T(1,128)S(1)}, f32[1,4096]{1,0:T(1,128)}, u32[]{:S(2)}) copy-start(f32[1,4096]{1,0:T(1,128)} %get-tuple-element.29) | copy-start | bytes 49156
  231.3 42.0 %copy-start.20 = (f32[1,4096]{1,0:T(1,128)S(1)}, f32[1,4096]{1,0:T(1,128)}, u32[]{:S(2)}) copy-start(f32[1,4096]{1,0:T(1,128)} %get-tuple-element.32) | copy-start | bytes 49156
  231.3 42.8 %copy-start.15 = (f32[1,4096]{1,0:T(1,128)S(1)}, f32[1,4096]{1,0:T(1,128)}, u32[]{:S(2)}) copy-start(f32[1,4096]{1,0:T(1,128)} %get-tuple-element.36) | copy-start | bytes 49156
  231.3 42.8 %copy-start.17 = (f32[1,4096]{1,0:T(1,128)S(1)}, f32[1,4096]{1,0:T(1,128)}, u32[]{:S(2)}) copy-start(f32[1,4096]{1,0:T(1,128)} %get-tuple-element.37) | copy-start | bytes 49156
  231.3 42.8 %copy-start.19 = (f32[1,4096]{1,0:T(1,128)S(1)}, f32[1,4096]{1,0:T(1,128)}, u32[]{:S(2)}) copy-start(f32[1,4096]{1,0:T(1,128)} %get-tuple-element.38) | copy-start | bytes 49156
  287.3 9.5 %copy-start.5 = (f32[2,8,32,128]{3,1,2,0:T(8,128)S(1)}, f32[2,8,32,128]{3,1,2,0:T(8,128)}, u32[]{:S(2)}) copy-start(f32[2,8,32,128]{3,1,2,0:T(8,128)} %copy-done.4) | copy-start | bytes 786436
  307.3 131.9 %copy-start.6 = (f32[1,16384]{1,0:T(1,128)S(1)}, f32[1,16384]{1,0:T(1,128)}, u32[]{:S(2)}) copy-start(f32[1,16384]{1,0:T(1,128)} %reshape.216.w_ref) | copy-start | bytes 196612
  585.1 267.2 %collective-permute-start.1 = (f32[1024,1024]{1,0:T(8,128)}, f32[1024,1024]{1,0:T(8,128)}, u32[]{:S(2)}, u32[]{:S(2)}) collective-permute-start(f32[1024,1024]{1,0:T(8,128)} %hidden_grad.3), channel_id=1, source_target_pairs={{0,8},{1,9},{2,10},{3,11},{4,12},{5,13},{6,14},{7,15},{8,0},{9,1},... | collective-permute-start | bytes 12582920 | tf_op jit(solution)/shard_map/ppermute | solution.py:315
  640.1 1.6 slice-start
  644.0 197.8 %collective-permute-start = (bf16[1024,960]{0,1:T(8,128)(2,1)}, bf16[1024,960]{0,1:T(8,128)(2,1)S(1)}, u32[]{:S(2)}, u32[]{:S(2)}) collective-permute-start(bf16[1024,960]{0,1:T(8,128)(2,1)} %copy.98), channel_id=1, source_target_pairs={{0,8},{1,9},{2,10},{3,11},{4,12},{5,13},{6,14},{7,15},{8,0},{9,1},... | collective-permute-start | bytes 5898248 | tf_op jit(solution)/shard_map/ppermute | solution.py:322
  829.6 14.8 %copy-start.24 = (pred[1024]{0:T(1024)(128)(4,1)S(1)}, pred[1024]{0:T(1024)(128)(4,1)}, u32[]{:S(2)}) copy-start(pred[1024]{0:T(1024)(128)(4,1)} %fusion.19) | copy-start | bytes 3076
  844.4 7.9 copy-start.1
  844.4 7.9 copy-start.8
  844.4 8.0 copy-start.10
  844.4 8.0 copy-start.12
  852.3 6.0 copy-start.25
  859.0 8.9 %copy-start.14 = (f32[1024]{0:T(1024)S(1)}, f32[1024]{0:T(1024)}, u32[]{:S(2)}) copy-start(f32[1024]{0:T(1024)} %copy-done.13) | copy-start | bytes 12292
Sparse Core Ops, SparseCore 0:
  28.5 49.5 all-gather.9
  80.3 48.6 all-gather.11
  131.2 48.6 all-gather.13
  182.6 48.6 all-gather.15
  233.6 230.5 all-gather.7
  466.3 137.3 all-gather.17

commit v2 on v1

--- a/solution.py
+++ b/solution.py
@@ -11,7 +11,7 @@
 F32 = jnp.float32
 BF16 = jnp.bfloat16
 VMEM_LIMIT = 60 * 1024 * 1024
-CHUNKS = 4
+CHUNKS = 2
 
 
 def layer_norm(inputs, ln_gain, ln_bias):
@@ -43,7 +43,7 @@
     s_ref[...] = s
 
 
-def logits_pass(e, z, carry, chunk, total, pt=512, sub=256):
+def logits_pass(e, z, carry, chunk, total, pt=1024, sub=256):
     n_v, dim = e.shape
     n_p = z.shape[0]
     steps = n_p // pt
@@ -199,6 +199,48 @@
         cost_estimate=pl.CostEstimate(flops=10**10, bytes_accessed=2 * n_b * n_p * dim, transcendentals=0),
         name="add_rows",
     )(counts, codes.reshape(n_b, 1, n_p), d_emb, grad)
+
+
+def place_rows_body(count_ref, code_ref, e_ref, out_ref, wide_ref, rows_ref):
+    b = pl.program_id(0)
+
+    @pl.when(b == 0)
+    def _():
+        wide_ref[...] = e_ref[...].astype(F32)
+
+    rows_ref[...] = jnp.zeros_like(rows_ref)
+
+    def step(k, carry):
+        code = code_ref[0, 0, k]
+        dst = lax.shift_right_logical(code, 12)
+        src = lax.bitwise_and(code, 4095)
+        rows_ref[pl.ds(dst, 1), :] = wide_ref[pl.ds(src, 1), :]
+        return carry
+
+    lax.fori_loop(0, count_ref[b], step, 0)
+    out_ref[...] = rows_ref[...].astype(BF16)
+
+
+def place_rows(counts, codes, e):
+    n_b, n_p = codes.shape
+    n_v, dim = e.shape
+    return pl.pallas_call(
+        place_rows_body,
+        grid_spec=pltpu.PrefetchScalarGridSpec(
+            num_scalar_prefetch=1,
+            grid=(n_b,),
+            in_specs=[
+                pl.BlockSpec((1, 1, n_p), lambda b, c: (b, 0, 0), memory_space=pltpu.SMEM),
+                pl.BlockSpec((n_v, dim), lambda b, c: (0, 0), pipeline_mode=pl.Buffered(1)),
+            ],
+            out_specs=pl.BlockSpec((n_p, dim), lambda b, c: (b, 0)),
+            scratch_shapes=[pltpu.VMEM((n_v, dim), F32), pltpu.VMEM((n_p, dim), F32)],
+        ),
+        out_shape=jax.ShapeDtypeStruct((n_b * n_p, dim), BF16),
+        compiler_params=pltpu.CompilerParams(vmem_limit_bytes=VMEM_LIMIT, dimension_semantics=("arbitrary",)),
+        cost_estimate=pl.CostEstimate(flops=10**10, bytes_accessed=2 * n_b * n_p * dim, transcendentals=0),
+        name="place_rows",
+    )(counts, codes.reshape(n_b, 1, n_p), e)
 
 
 def exchange_body(x_ref, out_ref, send_sem, recv_sem, *, axis, n_dev, split):
@@ -272,6 +314,16 @@
         normed, ln_vjp = jax.vjp(layer_norm, hid, ln_gain, ln_bias)
         z = normed.astype(BF16)
 
+        rel = tok_all - me * n_v
+        mine = (rel >= 0) & (rel < n_v)
+        upto = (jnp.arange(seq)[:, None] <= jnp.arange(seq)[None, :]).astype(BF16)
+        rank = jnp.dot(mine.astype(BF16), upto, preferred_element_type=F32).astype(jnp.int32) - 1
+        code = jnp.where(mine, jnp.arange(seq, dtype=jnp.int32)[None, :] * 4096 + rel, 0)
+        slot = jnp.where(mine, rank, -1)
+        codes = jnp.sum(jnp.where(slot[:, :, None] == jnp.arange(seq, dtype=jnp.int32)[None, None, :], code[:, :, None], 0), axis=1)
+        counts = jnp.sum(mine.astype(jnp.int32), axis=1)
+        emb_part = place_rows(counts, codes, table_shard)
+
         carry = None
         maxes, sums, z_parts = [], [], []
         for c in range(CHUNKS):
@@ -311,26 +363,14 @@
         def half_grad(d, z_d):
             return hidden_grad(half_base.reshape(1), z_d, e_half, row_of(lse_all, d)[:, None], row_of(weight_all, d)[:, None], row_of(label_all, d)[:, None])
 
+        z_other, d_table = lax.optimization_barrier((z_other, d_table))
         dz_other = half_grad(other, z_other)
+        emb_part, dz_other = lax.optimization_barrier((emb_part, dz_other))
+        emb_rows = lax.psum_scatter(emb_part, 'fsdp', scatter_dimension=0, tiled=True).reshape(1, seq, dim)
         dz_other = lax.ppermute(dz_other, 'fsdp', partner)
         dz_own = half_grad(me, z)
 
-        tok_own = row_of(tok_all, me)
-        in_half = (tok_own // (half * n_v)) == plane
-        look = jnp.concatenate([row_of(tok_all, other), tok_own]) - half_base
-        found = jnp.take(e_half, jnp.clip(look, 0, half * n_v - 1), axis=0, mode='clip')
-        found_other = lax.ppermute(found[:seq], 'fsdp', partner)
-        emb_rows = jnp.where(in_half[:, None], found[seq:], found_other).reshape(1, seq, dim)
-
         de_all = lax.all_gather(d_emb.reshape(seq, dim), 'fsdp', axis=0, tiled=True)
-        rel = tok_all - me * n_v
-        mine = (rel >= 0) & (rel < n_v)
-        upto = (jnp.arange(seq)[:, None] <= jnp.arange(seq)[None, :]).astype(BF16)
-        rank = jnp.dot(mine.astype(BF16), upto, preferred_element_type=F32).astype(jnp.int32) - 1
-        code = jnp.where(mine, jnp.arange(seq, dtype=jnp.int32)[None, :] * 4096 + rel, 0)
-        slot = jnp.where(mine, rank, -1)
-        codes = jnp.sum(jnp.where(slot[:, :, None] == jnp.arange(seq, dtype=jnp.int32)[None, None, :], code[:, :, None], 0), axis=1)
-        counts = jnp.sum(mine.astype(jnp.int32), axis=1)
         d_table, dz_own = lax.optimization_barrier((d_table, dz_own))
         d_table = add_rows(counts, codes, de_all, d_table)
 

time: 889 us -> 916 us (1.030)
  waiting for transfers between devices: 69 us -> 189 us
  local copies, waits for them, and re-layouts: 116 us -> 54.4 us
  starting transfers between devices: 31.3 us -> 1.36 us
    reduce_scatter x0 -> x1, waiting for transfers between devices: none -> 156 us  [device_step(): lax.psum_scatter(emb_part, 'fsdp', scatter_dimension=0, tiled=True)]
    gather x1 -> x0, local copies, waits for them, and re-layouts: 53.5 us -> none  [device_step(): jnp.take(e_half, jnp.clip(look, 0, half * n_v - 1), axis=0, mode='clip')]
    pallas_call x0 -> x1, Pallas kernels: none -> 31.1 us  [place_rows(): pl.pallas_call(place_rows_body, grid_spec=pltpu.PrefetchScalarGridSpec(nu...]
    ppermute x1 -> x0, starting transfers between devices: 29.1 us -> none  [device_step(): found_other = lax.ppermute(found[:seq], 'fsdp', partner)]
    pallas_call x4 -> x2, Pallas kernels: 168 us -> 142 us  [logits_pass(): pl.pallas_call(functools.partial(logits_body, sub=sub, n_sub=n_v // sub),...]
    all_gather x4 -> x2, waiting for transfers between devices: 51.5 us -> 28.8 us  [device_step(): z_c = lax.all_gather(z[c * part:(c + 1) * part], 'fsdp', axis=0, tiled=True)]
    all_gather x1, waiting for transfers between devices: 15.5 us -> 0.01 us  [device_step(): lax.all_gather(table_shard, 'fsdp', axis=0, tiled=True, axis_index_groups...]
    unnamed x64 -> x50, local copies, waits for them, and re-layouts: 36.8 us -> 37.4 us
  transfers between devices with their start and end apart: 8 -> 6, of which waited for: 5 -> 4; matrix products, arithmetic and copies ran while one was open for 14% -> 8% of each run, Pallas kernels for 67% -> 67%
where the time goes in v2:
time: 916 us; the launch traced here: 910 us
  Pallas kernels  620 us (68%)
  waiting for transfers between devices  189 us (21%)
  local copies, waits for them, and re-layouts  54.4 us (6%)
  other arithmetic  29.2 us (3%)
  between operations  16.9 us (2%)
    pallas_call x2, Pallas kernels, hidden_grad(): pl.pallas_call(functools.partial(hidden_grad_body, tp=tp, n_tp=n_p // tp,...  242 us
    reduce_scatter x1, waiting for transfers between devices, device_step(): lax.psum_scatter(emb_part, 'fsdp', scatter_dimension=0, tiled=True)  156 us
    pallas_call x2, Pallas kernels, logits_pass(): pl.pallas_call(functools.partial(logits_body, sub=sub, n_sub=n_v // sub),...  142 us
    pallas_call x1, Pallas kernels, table_grad(): pl.pallas_call(functools.partial(table_grad_body, sub=sub, n_sub=n_v // s...  132 us
    unnamed x50, local copies, waits for them, and re-layouts  37.4 us
    pallas_call x4, Pallas kernels, exchange(): pl.pallas_call(functools.partial(exchange_body, axis=axis, n_dev=n_dev, s...  36.6 us
    pallas_call x1, Pallas kernels, add_rows(): pl.pallas_call(add_rows_body, grid_spec=pltpu.PrefetchScalarGridSpec(num_...  36.2 us
    pallas_call x1, Pallas kernels, place_rows(): pl.pallas_call(place_rows_body, grid_spec=pltpu.PrefetchScalarGridSpec(nu...  31.1 us
  transfers between devices with their start and end apart: 6, of which 4 were waited for; matrix products, arithmetic and copies ran while one was open for 8% of the time, Pallas kernels for 67%

profile of v2, /device:TPU:0, one launch (start us, length us, event | category | flops | bytes accessed | tf_op | source)
XLA Modules:
  0.0 910.4 jit_solution(9932855258319686139)
XLA Ops:
  7.3 2.8 copy.55
  10.5 0.7 fusion.10
  11.4 0.6 pad_bitcast_fusion.x_ref
  12.0 11.3 %exchange.4 = f32[16,32,128]{2,1,0:T(8,128)} custom-call(f32[1,32,128]{2,1,0:T(8,128)} %pad_bitcast_fusion.x_ref), custom_call_target="tpu_custom_call" | custom-call | flops 4000000000 | tf_op jit(solution)/shard_map/exchange/pallas_call | solution.py:272
  23.4 1.1 copy.87
  24.8 0.8 fusion.8.z_ref
  25.6 1.3 copy-done.2
  26.9 1.5 fusion.20
  28.5 0.7 all-gather.8.cloned.1.call-update
  29.2 8.5 copy.54.e_ref.refs_0_
  37.8 1.5 copy-done.3
  39.3 2.5 copy.72
  41.8 0.6 reduce-scatter.2.cloned.1.call-start
  42.8 8.8 select_reduce_fusion
  51.6 0.7 reshape.147.code_ref
  52.3 0.6 convert_reduce_fusion.1.count_ref
  52.9 0.6 slice_reduce_fusion
  53.5 31.1 %place_rows.1 = bf16[16384,960]{1,0:T(8,128)(2,1)} custom-call(s32[16]{0:T(128)} %convert_reduce_fusion.1.count_ref, s32[16,1,1024]{2,1,0:T(1,128)} %reshape.147.code_ref, bf16[3072,960]{1,0:T(8,128)(2,1)} %copy.54.e_ref.refs_0_), custom_call_target="tpu_custom_call" | custom-call | flops 10000000000 | bytes 31457280 | tf_op jit(solution)/shard_map/place_rows/pallas_call | solution.py:227
  84.6 20.9 %all-gather.6.cloned.1.call-done.refs_1_ = bf16[8192,960]{1,0:T(8,128)(2,1)} async-done(((bf16[512,960]{1,0:T(8,128)(2,1)}), bf16[8192,960]{1,0:T(8,128)(2,1)}) %all-gather.6.cloned.1.call-update) | async-done | bytes 15728656 | tf_op jit(solution)/shard_map/all_gather | solution.py:330
  105.5 71.0 %logits_pass.2 = (f32[3072,16384]{1,0:T(8,128)}, bf16[16384,960]{1,0:T(8,128)(2,1)}, f32[1,8192]{1,0:T(1,128)}, f32[1,8192]{1,0:T(1,128)}) custom-call(bf16[3072,960]{1,0:T(8,128)(2,1)} %copy.54.e_ref.refs_0_, bf16[8192,960]{1,0:T(8,128)(2,1)} %all-gather.6.cloned.1.call-done.refs_1_), custom_call_target="tpu_custom_call" | custom-call | flops 48318382080 | bytes 106561536 | tf_op jit(solution)/shard_map/logits_pass/pallas_call | solution.py:58
  176.5 7.9 all-gather.8.cloned.1.call-done.refs_1_
  184.4 71.3 %logits_pass.3 = (f32[3072,16384]{1,0:T(8,128)}, bf16[16384,960]{1,0:T(8,128)(2,1)}, f32[1,8192]{1,0:T(1,128)}, f32[1,8192]{1,0:T(1,128)}) custom-call(bf16[3072,960]{1,0:T(8,128)(2,1)} %copy.54.e_ref.refs_0_, bf16[8192,960]{1,0:T(8,128)(2,1)} %all-gather.8.cloned.1.call-done.refs_1_, ...), custom_call_target="tpu_custom_call", output_to_operand_aliasing={{0}: (2, {}), {1}: (3, {})} | custom-call | flops 48318382080 | bytes 106561536 | tf_op jit(solution)/shard_map/logits_pass/pallas_call | solution.py:58
  255.7 0.8 pad_maximum_fusion.2
  256.6 0.8 pad_maximum_fusion.3
  257.5 0.7 pad_maximum_fusion.1.x_ref
  258.1 9.0 exchange.5
  267.1 0.9 slice_reduce_fusion.1
  268.0 0.9 multiply_reduce_fusion.2
  268.9 0.6 add_bitcast_fusion.x_ref
  269.5 7.8 exchange.6
  277.3 0.9 reshape_reshape.3
  278.1 0.9 copy.88
  279.0 2.1 multiply_reduce_fusion.1
  281.1 0.7 reshape.154.w_ref
  281.8 0.7 reshape.156.y_ref
  282.5 0.7 reshape.152.lse_ref
  283.2 1.3 constant_dynamic-slice_fusion
  284.5 1.3 constant_dynamic-slice_fusion.1
  285.8 1.6 pad_maximum_fusion.z_ref
  287.4 131.9 %table_grad.1 = (f32[3072,960]{1,0:T(8,128)}, f32[1,16384]{1,0:T(1,128)}) custom-call(s32[1]{0:T(128)} %bitcast.6.base_ref, f32[3072,16384]{1,0:T(8,128)} %get-tuple-element.24.lt_ref, bf16[16384,960]{1,0:T(8,128)(2,1)} %get-tuple-element.25.z_ref, f32[1,16384]{1,0:T(1,128)} %reshape.152.lse_ref, f32[1,16384]{1,0:T(1,128)} %reshape.154.w_ref, ...), custom_call_target="tpu_custom_call" | custom-call | flops 96636764160 | bytes 201326592 | tf_op jit(solution)/shard_map/table_grad/pallas_call | solution.py:107
  419.4 1.0 copy.66.lse_ref
  420.4 1.0 copy.67.w_ref
  421.4 1.0 copy.68.y_ref
  422.5 120.9 %hidden_grad.2 = f32[1024,1024]{1,0:T(8,128)} custom-call(s32[1]{0:T(128)} %bitcast.4.base_ref, bf16[1024,960]{1,0:T(8,128)(2,1)} %pad_maximum_fusion.z_ref, bf16[24576,960]{1,0:T(8,128)(2,1)} %all-gather.10.cloned.1.call-done.e_ref, f32[1024,1]{1,0:T(8,128)} %copy.66.lse_ref, f32[1024,1]{1,0:T(8,128)} %copy.67.w_ref, s32[1024,1]{1,0:T(8,128)} %copy.68.y_ref), custom_call_target="tpu_custom_call" | custom-call | flops 96636764160 | bytes 47185920 | tf_op jit(solution)/shard_map/hidden_grad/pallas_call | solution.py:146
  543.4 1.0 copy.69.lse_ref
  544.5 1.0 copy.70.w_ref
  545.5 1.0 copy.71.y_ref
  546.5 0.7 multiply_reduce_fusion
  547.2 0.6 broadcast_in_dim.63
  548.0 0.6 collective-permute-start
  548.6 120.7 %hidden_grad.3 = f32[1024,1024]{1,0:T(8,128)} custom-call(s32[1]{0:T(128)} %bitcast.4.base_ref, bf16[1024,960]{1,0:T(8,128)(2,1)} %copy-done.2, bf16[24576,960]{1,0:T(8,128)(2,1)} %all-gather.10.cloned.1.call-done.e_ref, f32[1024,1]{1,0:T(8,128)} %copy.69.lse_ref, f32[1024,1]{1,0:T(8,128)} %copy.70.w_ref, s32[1024,1]{1,0:T(8,128)} %copy.71.y_ref), custom_call_target="tpu_custom_call" | custom-call | flops 96636764160 | bytes 47185920 | tf_op jit(solution)/shard_map/hidden_grad/pallas_call | solution.py:146
  669.3 36.2 %add_rows.1 = f32[3072,960]{1,0:T(8,128)} custom-call(s32[16]{0:T(128)} %convert_reduce_fusion.1.count_ref, s32[16,1,1024]{2,1,0:T(1,128)} %reshape.147.code_ref, bf16[16384,960]{1,0:T(8,128)(2,1)} %bitcast.93, f32[3072,960]{1,0:T(8,128)} %get-tuple-element.37.grad_ref), custom_call_target="tpu_custom_call" | custom-call | flops 10000000000 | bytes 31457280 | tf_op jit(solution)/shard_map/add_rows/pallas_call | solution.py:184
  705.5 12.4 %copy.75 = f32[3072,960]{0,1:T(8,128)} copy(f32[3072,960]{1,0:T(8,128)} %add_rows.1) | data formatting | bytes 23592960
  717.9 3.0 collective-permute-done
  721.0 4.6 fusion.11
  725.6 1.8 fusion.19
  727.7 2.4 copy.74
  730.2 0.7 maximum_maximum_fusion
  730.9 8.5 exchange.7
  739.4 0.7 reduce_sum.145
  740.2 0.6 slice.56
  741.9 0.6 slice_bitcast_fusion
  742.5 156.0 %reduce-scatter.2.cloned.1.call-done = bf16[1024,960]{1,0:T(8,128)(2,1)} async-done(((bf16[16384,960]{1,0:T(8,128)(2,1)}), bf16[1024,960]{1,0:T(8,128)(2,1)}) %reduce-scatter.2.cloned.1.call-update) | async-done | bytes 1966096 | tf_op jit(solution)/shard_map/reduce_scatter | solution.py:369
  898.5 3.9 copy.73
  (76 shorter events, 2.1 us)
Async XLA Ops:
  7.2 4.1 copy-start.16
  7.2 4.1 copy-start.17
  7.2 4.1 copy-start.18
  7.2 4.1 copy-start.19
  7.2 4.1 copy-start.20
  7.2 98.3 %all-gather.6.cloned.1.call-start = ((), (), s32[]{:S(2)}) async-start(), calls=%async_computation.1 | async-start | bytes 17825792 | tf_op jit(solution)/shard_map/all_gather | solution.py:330
  10.1 14.6 %copy-start = (bf16[1,1024,960]{2,1,0:T(8,128)(2,1)}, bf16[1,1024,960]{2,1,0:T(8,128)(2,1)S(1)}, u32[]{:S(2)}) copy-start(bf16[1,1024,960]{2,1,0:T(8,128)(2,1)S(1)} %copy.55) | copy-start | bytes 5898244
  10.5 14.3 %copy-start.5 = (f32[1024]{0:T(1024)}, f32[1024]{0:T(1024)S(1)}, u32[]{:S(2)}) copy-start(f32[1024]{0:T(1024)S(1)} %broadcast_multiply_fusion) | copy-start | bytes 12292
  11.2 12.2 %copy-start.12 = (f32[1024]{0:T(1024)}, f32[1024]{0:T(1024)S(1)}, u32[]{:S(2)}) copy-start(f32[1024]{0:T(1024)S(1)} %fusion.10) | copy-start | bytes 12292
  11.2 13.5 %copy-start.10 = (f32[1024]{0:T(1024)}, f32[1024]{0:T(1024)S(1)}, u32[]{:S(2)}) copy-start(f32[1024]{0:T(1024)S(1)} %fusion.18) | copy-start | bytes 12292
  24.6 3.7 copy-start.8
  25.6 1.3 copy-start.2
  28.4 156.0 %all-gather.8.cloned.1.call-start = ((), (), s32[]{:S(2)}) async-start(), calls=%async_computation.2 | async-start | bytes 17825792 | tf_op jit(solution)/shard_map/all_gather | solution.py:330
  29.2 393.3 %all-gather.10.cloned.1.call-start = ((), (), s32[]{:S(2)}) async-start(), calls=%async_computation.3 | async-start | bytes 56623104 | tf_op jit(solution)/shard_map/all_gather | solution.py:357
  37.7 1.5 copy-start.3
  37.8 631.5 %all-gather.12.cloned.1.call-start = ((), (), s32[]{:S(2)}) async-start(), calls=%async_computation.5 | async-start | bytes 35651584 | tf_op jit(solution)/shard_map/all_gather | solution.py:373
  41.8 856.7 %reduce-scatter.2.cloned.1.call-start = ((), (), s32[]{:S(2)}) async-start(), calls=%async_computation.4 | async-start | bytes 35651584 | tf_op jit(solution)/shard_map/reduce_scatter | solution.py:369
  184.4 71.3 %copy-start.15 = (f32[1,8192]{1,0:T(1,128)S(1)}, f32[1,8192]{1,0:T(1,128)}, u32[]{:S(2)}) copy-start(f32[1,8192]{1,0:T(1,128)} %get-tuple-element.26) | copy-start | bytes 98308
  184.4 72.2 %copy-start.14 = (f32[1,8192]{1,0:T(1,128)S(1)}, f32[1,8192]{1,0:T(1,128)}, u32[]{:S(2)}) copy-start(f32[1,8192]{1,0:T(1,128)} %get-tuple-element.28) | copy-start | bytes 98308
  543.4 3.1 copy-start.4
  543.4 3.1 copy-start.7
  548.0 173.0 %collective-permute-start = (f32[1024,1024]{1,0:T(8,128)}, f32[1024,1024]{1,0:T(8,128)}, u32[]{:S(2)}, u32[]{:S(2)}) collective-permute-start(f32[1024,1024]{1,0:T(8,128)} %hidden_grad.2), channel_id=1, source_target_pairs={{0,8},{1,9},{2,10},{3,11},{4,12},{5,13},{6,14},{7,15},{8,0},{9,1},... | collective-permute-start | bytes 12582920 | tf_op jit(solution)/shard_map/ppermute | solution.py:370
  705.5 15.5 %copy-start.1 = (bf16[1,1024,960]{2,1,0:T(8,128)(2,1)S(1)}, bf16[1,1024,960]{2,1,0:T(8,128)(2,1)}, u32[]{:S(2)}) copy-start(bf16[1,1024,960]{2,1,0:T(8,128)(2,1)} %copy-done) | copy-start | bytes 5898244
  705.5 15.5 %copy-start.6 = (f32[1024]{0:T(1024)S(1)}, f32[1024]{0:T(1024)}, u32[]{:S(2)}) copy-start(f32[1024]{0:T(1024)} %copy-done.5) | copy-start | bytes 12292
  705.5 15.5 %copy-start.9 = (f32[960]{0:T(1024)S(1)}, f32[960]{0:T(1024)}, u32[]{:S(2)}) copy-start(f32[960]{0:T(1024)} %copy-done.8) | copy-start | bytes 11524
  705.5 15.5 %copy-start.11 = (f32[1024]{0:T(1024)S(1)}, f32[1024]{0:T(1024)}, u32[]{:S(2)}) copy-start(f32[1024]{0:T(1024)} %copy-done.10) | copy-start | bytes 12292
  717.9 7.7 copy-start.13
Sparse Core Ops, SparseCore 0:
  28.5 76.9 all-gather.5
  108.3 76.0 all-gather.7
  186.9 229.8 all-gather.9
  418.8 131.2 all-gather.11
  552.3 346.1 reduce-scatter.1

commit v3 on v2

--- a/solution.py
+++ b/solution.py
@@ -201,46 +201,57 @@
     )(counts, codes.reshape(n_b, 1, n_p), d_emb, grad)
 
 
-def place_rows_body(count_ref, code_ref, e_ref, out_ref, wide_ref, rows_ref):
+def place_rows_body(count_ref, code_ref, e_ref, first_ref, second_ref, wide_ref, rows_ref):
     b = pl.program_id(0)
+    n_b = pl.num_programs(0)
+    n_p = first_ref.shape[0]
 
     @pl.when(b == 0)
     def _():
-        wide_ref[...] = e_ref[...].astype(F32)
-
-    rows_ref[...] = jnp.zeros_like(rows_ref)
-
-    def step(k, carry):
-        code = code_ref[0, 0, k]
-        dst = lax.shift_right_logical(code, 12)
-        src = lax.bitwise_and(code, 4095)
-        rows_ref[pl.ds(dst, 1), :] = wide_ref[pl.ds(src, 1), :]
-        return carry
-
-    lax.fori_loop(0, count_ref[b], step, 0)
-    out_ref[...] = rows_ref[...].astype(BF16)
+        rows_ref[...] = jnp.zeros_like(rows_ref)
+
+    wide_ref[...] = e_ref[...].astype(F32)
+
+    for part in range(2):
+        def step(k, carry):
+            code = code_ref[0, part, k]
+            dst = lax.shift_right_logical(code, 12) + part * n_p
+            src = lax.bitwise_and(code, 4095)
+            rows_ref[pl.ds(dst, 1), :] = wide_ref[pl.ds(src, 1), :]
+            return carry
+
+        lax.fori_loop(0, count_ref[part * n_b + b], step, 0)
+
+    @pl.when(b == n_b - 1)
+    def _():
+        dim = rows_ref.shape[1]
+        first_ref[:, :dim] = rows_ref[:n_p, :].astype(BF16)
+        second_ref[:, :dim] = rows_ref[n_p:, :].astype(BF16)
 
 
 def place_rows(counts, codes, e):
-    n_b, n_p = codes.shape
-    n_v, dim = e.shape
+    _, n_b, n_p = codes.shape
+    dim = e.shape[1]
+    n_v = e.shape[0] // n_b
+    wide = pl.cdiv(dim, 128) * 128
+    out = pl.BlockSpec((n_p, wide), lambda b, c: (0, 0), pipeline_mode=pl.Buffered(1))
     return pl.pallas_call(
         place_rows_body,
         grid_spec=pltpu.PrefetchScalarGridSpec(
             num_scalar_prefetch=1,
             grid=(n_b,),
             in_specs=[
-                pl.BlockSpec((1, 1, n_p), lambda b, c: (b, 0, 0), memory_space=pltpu.SMEM),
-                pl.BlockSpec((n_v, dim), lambda b, c: (0, 0), pipeline_mode=pl.Buffered(1)),
+                pl.BlockSpec((1, 2, n_p), lambda b, c: (b, 0, 0), memory_space=pltpu.SMEM),
+                pl.BlockSpec((n_v, dim), lambda b, c: (b, 0)),
             ],
-            out_specs=pl.BlockSpec((n_p, dim), lambda b, c: (b, 0)),
-            scratch_shapes=[pltpu.VMEM((n_v, dim), F32), pltpu.VMEM((n_p, dim), F32)],
+            out_specs=[out, out],
+            scratch_shapes=[pltpu.VMEM((n_v, dim), F32), pltpu.VMEM((2 * n_p, dim), F32)],
         ),
-        out_shape=jax.ShapeDtypeStruct((n_b * n_p, dim), BF16),
+        out_shape=[jax.ShapeDtypeStruct((n_p, wide), BF16)] * 2,
         compiler_params=pltpu.CompilerParams(vmem_limit_bytes=VMEM_LIMIT, dimension_semantics=("arbitrary",)),
-        cost_estimate=pl.CostEstimate(flops=10**10, bytes_accessed=2 * n_b * n_p * dim, transcendentals=0),
+        cost_estimate=pl.CostEstimate(flops=10**10, bytes_accessed=2 * n_b * n_v * dim, transcendentals=0),
         name="place_rows",
-    )(counts, codes.reshape(n_b, 1, n_p), e)
+    )(counts.reshape(-1), codes.transpose(1, 0, 2), e)
 
 
 def exchange_body(x_ref, out_ref, send_sem, recv_sem, *, axis, n_dev, split):
@@ -314,20 +325,32 @@
         normed, ln_vjp = jax.vjp(layer_norm, hid, ln_gain, ln_bias)
         z = normed.astype(BF16)
 
-        rel = tok_all - me * n_v
-        mine = (rel >= 0) & (rel < n_v)
+        def row_of(a, d):
+            return lax.dynamic_index_in_dim(a, d, 0, keepdims=False)
+
         upto = (jnp.arange(seq)[:, None] <= jnp.arange(seq)[None, :]).astype(BF16)
-        rank = jnp.dot(mine.astype(BF16), upto, preferred_element_type=F32).astype(jnp.int32) - 1
-        code = jnp.where(mine, jnp.arange(seq, dtype=jnp.int32)[None, :] * 4096 + rel, 0)
-        slot = jnp.where(mine, rank, -1)
-        codes = jnp.sum(jnp.where(slot[:, :, None] == jnp.arange(seq, dtype=jnp.int32)[None, None, :], code[:, :, None], 0), axis=1)
-        counts = jnp.sum(mine.astype(jnp.int32), axis=1)
-        emb_part = place_rows(counts, codes, table_shard)
+
+        def pack(rel):
+            hit = (rel >= 0) & (rel < n_v)
+            rank = jnp.dot(hit.astype(BF16), upto, preferred_element_type=F32).astype(jnp.int32) - 1
+            code = jnp.where(hit, jnp.arange(seq, dtype=jnp.int32)[None, :] * 4096 + rel, 0)
+            slot = jnp.where(hit, rank, -1)
+            codes = jnp.sum(jnp.where(slot[:, :, None] == jnp.arange(seq, dtype=jnp.int32)[None, None, :], code[:, :, None], 0), axis=1)
+            return codes, jnp.sum(hit.astype(jnp.int32), axis=1)
+
+        codes, counts = pack(tok_all - me * n_v)
+        tok_own = row_of(tok_all, me)
+        block_start = (plane * half + jnp.arange(half, dtype=jnp.int32)) * n_v
+        look = jnp.stack([row_of(tok_all, other), tok_own])[:, None, :] - block_start[None, :, None]
+        look_codes, look_counts = pack(look.reshape(2 * half, seq))
+        in_half = (tok_own // (half * n_v)) == plane
 
         carry = None
         maxes, sums, z_parts = [], [], []
         for c in range(CHUNKS):
             z_c = lax.all_gather(z[c * part:(c + 1) * part], 'fsdp', axis=0, tiled=True)
+            if c == 0:
+                z_c, codes, counts, look_codes, look_counts = lax.optimization_barrier((z_c, codes, counts, look_codes, look_counts))
             lt, z_all, m_c, s_c = logits_pass(table_shard, z_c, carry, c, total)
             carry = (lt, z_all)
             maxes.append(m_c)
@@ -357,18 +380,17 @@
         e_half = lax.all_gather(table_shard, 'fsdp', axis=0, tiled=True, axis_index_groups=planes)
         half_base = (plane * half * n_v).astype(jnp.int32)
 
-        def row_of(a, d):
-            return lax.dynamic_index_in_dim(a, d, 0, keepdims=False)
-
         def half_grad(d, z_d):
             return hidden_grad(half_base.reshape(1), z_d, e_half, row_of(lse_all, d)[:, None], row_of(weight_all, d)[:, None], row_of(label_all, d)[:, None])
 
         z_other, d_table = lax.optimization_barrier((z_other, d_table))
         dz_other = half_grad(other, z_other)
-        emb_part, dz_other = lax.optimization_barrier((emb_part, dz_other))
-        emb_rows = lax.psum_scatter(emb_part, 'fsdp', scatter_dimension=0, tiled=True).reshape(1, seq, dim)
         dz_other = lax.ppermute(dz_other, 'fsdp', partner)
+        found_other, found_own = place_rows(look_counts, look_codes.reshape(2, half, seq), e_half)
+        found_other, z = lax.optimization_barrier((found_other, z))
+        found_other = lax.ppermute(found_other, 'fsdp', partner)
         dz_own = half_grad(me, z)
+        emb_rows = jnp.where(in_half[:, None], found_own[:, :dim], found_other[:, :dim]).reshape(1, seq, dim)
 
         de_all = lax.all_gather(d_emb.reshape(seq, dim), 'fsdp', axis=0, tiled=True)
         d_table, dz_own = lax.optimization_barrier((d_table, dz_own))

time: 916 us -> 798 us (0.87)
  waiting for transfers between devices: 189 us -> 50.4 us
  other arithmetic: 29.2 us -> 49.2 us
    reduce_scatter x1 -> x0, waiting for transfers between devices: 156 us -> none  [device_step(): lax.psum_scatter(emb_part, 'fsdp', scatter_dimension=0, tiled=True)]
    all_gather x2, waiting for transfers between devices: 28.8 us -> 49.6 us  [device_step(): z_c = lax.all_gather(z[c * part:(c + 1) * part], 'fsdp', axis=0, tiled=True)]
    reduce_sum x2 -> x4, other arithmetic: 9.43 us -> 19 us  [the longest x2 18.2 us: pack(): jnp.sum(jnp.where(slot[:, :, None] == jnp.arange(seq, dtype=jnp.int32)[No...]
    unnamed x50 -> x46, local copies, waits for them, and re-layouts: 37.4 us -> 37.6 us
  transfers between devices with their start and end apart: 6 -> 6, of which waited for: 4 -> 2; matrix products, arithmetic and copies ran while one was open for 8% -> 10% of each run, Pallas kernels for 67% -> 75%
where the time goes in v3:
time: 798 us; the launch traced here: 793 us
  Pallas kernels  616 us (77%)
  local copies, waits for them, and re-layouts  57.3 us (7%)
  waiting for transfers between devices  50.4 us (6%)
  other arithmetic  49.2 us (6%)
  between operations  16.8 us (2%)
    pallas_call x2, Pallas kernels, hidden_grad(): pl.pallas_call(functools.partial(hidden_grad_body, tp=tp, n_tp=n_p // tp,...  242 us
    pallas_call x2, Pallas kernels, logits_pass(): pl.pallas_call(functools.partial(logits_body, sub=sub, n_sub=n_v // sub),...  142 us
    pallas_call x1, Pallas kernels, table_grad(): pl.pallas_call(functools.partial(table_grad_body, sub=sub, n_sub=n_v // s...  132 us
    all_gather x2, waiting for transfers between devices, device_step(): z_c = lax.all_gather(z[c * part:(c + 1) * part], 'fsdp', axis=0, tiled=True)  49.6 us
    unnamed x46, local copies, waits for them, and re-layouts  37.6 us
    pallas_call x1, Pallas kernels, add_rows(): pl.pallas_call(add_rows_body, grid_spec=pltpu.PrefetchScalarGridSpec(num_...  36 us
    pallas_call x4, Pallas kernels, exchange(): pl.pallas_call(functools.partial(exchange_body, axis=axis, n_dev=n_dev, s...  35 us
    pallas_call x1, Pallas kernels, place_rows(): pl.pallas_call(place_rows_body, grid_spec=pltpu.PrefetchScalarGridSpec(nu...  29.1 us
  transfers between devices with their start and end apart: 6, of which 2 were waited for; matrix products, arithmetic and copies ran while one was open for 10% of the time, Pallas kernels for 75%

profile of v3, /device:TPU:0, one launch (start us, length us, event | category | flops | bytes accessed | tf_op | source)
XLA Modules:
  0.0 793.1 jit_solution(12209674786502116156)
XLA Ops:
  7.2 0.7 convert_element_type.54
  7.9 0.7 convert_element_type.56
  8.6 0.7 convert_element_type.58
  9.3 0.7 concatenate.12
  10.6 11.3 %exchange.4 = f32[16,32,128]{2,1,0:T(8,128)} custom-call(f32[1,32,128]{2,1,0:T(8,128)} %pad_bitcast_fusion.x_ref), custom_call_target="tpu_custom_call" | custom-call | flops 4000000000 | tf_op jit(solution)/shard_map/exchange/pallas_call | solution.py:283
  22.0 1.1 copy.87
  23.1 2.8 copy.53
  26.3 0.7 fusion.10
  27.8 0.8 fusion.8.z_ref
  28.7 1.6 fusion.32
  30.7 0.7 all-gather.10.cloned.1.call-update
  31.5 8.5 %copy.55.refs_0_ = bf16[3072,960]{1,0:T(8,128)(2,1)} copy(bf16[3072,960]{0,1:T(8,128)(2,1)} %param.13) | data formatting | bytes 11796480 | tf_op args[5]
  40.6 0.9 copy-done.4
  41.6 2.5 copy.71
  44.3 0.6 slice_reduce_fusion
  46.8 0.6 convert_reduce_fusion.2
  47.8 8.8 %select_reduce_fusion = s32[16,1024]{1,0:T(8,128)S(1)} fusion(s32[16,1024]{1,0:T(8,128)S(1)} %get-tuple-element.96, s32[16,1024]{1,0:T(8,128)S(1)} %fusion.21), kind=kLoop, calls=%fused_computation | loop fusion | flops 50315264 | bytes 196608 | tf_op jit(solution)/shard_map/reduce_sum | solution.py:338
  56.6 9.4 %select_reduce_fusion.1 = s32[16,1024]{1,0:T(8,128)} fusion(s32[16,1024]{1,0:T(8,128)S(1)} %get-tuple-element.97, s32[16,1024]{1,0:T(8,128)S(1)} %fusion.18), kind=kLoop, calls=%fused_computation.2 | loop fusion | flops 50315264 | bytes 196608 | tf_op jit(solution)/shard_map/reduce_sum | solution.py:338
  66.0 41.7 %all-gather.6.cloned.1.call-done.refs_1_ = bf16[8192,960]{1,0:T(8,128)(2,1)} async-done(((bf16[512,960]{1,0:T(8,128)(2,1)}), bf16[8192,960]{1,0:T(8,128)(2,1)}) %all-gather.6.cloned.1.call-update) | async-done | bytes 15728656 | tf_op jit(solution)/shard_map/all_gather | solution.py:351
  107.7 71.0 %logits_pass.2 = (f32[3072,16384]{1,0:T(8,128)}, bf16[16384,960]{1,0:T(8,128)(2,1)}, f32[1,8192]{1,0:T(1,128)}, f32[1,8192]{1,0:T(1,128)}) custom-call(bf16[3072,960]{1,0:T(8,128)(2,1)} %copy.55.refs_0_, bf16[8192,960]{1,0:T(8,128)(2,1)} %all-gather.6.cloned.1.call-done.refs_1_), custom_call_target="tpu_custom_call" | custom-call | flops 48318382080 | bytes 106561536 | tf_op jit(solution)/shard_map/logits_pass/pallas_call | solution.py:58
  178.7 7.9 all-gather.10.cloned.1.call-done.refs_1_
  186.6 71.3 %logits_pass.3 = (f32[3072,16384]{1,0:T(8,128)}, bf16[16384,960]{1,0:T(8,128)(2,1)}, f32[1,8192]{1,0:T(1,128)}, f32[1,8192]{1,0:T(1,128)}) custom-call(bf16[3072,960]{1,0:T(8,128)(2,1)} %copy.55.refs_0_, bf16[8192,960]{1,0:T(8,128)(2,1)} %all-gather.10.cloned.1.call-done.refs_1_, ...), custom_call_target="tpu_custom_call", output_to_operand_aliasing={{0}: (2, {}), {1}: (3, {})} | custom-call | flops 48318382080 | bytes 106561536 | tf_op jit(solution)/shard_map/logits_pass/pallas_call | solution.py:58
  257.9 0.8 pad_maximum_fusion.2
  258.8 0.8 pad_maximum_fusion.3
  259.7 0.7 pad_maximum_fusion.1.x_ref
  260.4 9.0 %exchange.5 = f32[16,16,128]{2,1,0:T(8,128)} custom-call(f32[16,16,128]{2,1,0:T(8,128)} %pad_maximum_fusion.1.x_ref), custom_call_target="tpu_custom_call" | custom-call | flops 4000000000 | tf_op jit(solution)/shard_map/exchange/pallas_call | solution.py:283
  269.3 0.9 slice_reduce_fusion.1
  270.2 0.9 multiply_reduce_fusion.2
  271.7 7.7 exchange.6
  279.5 0.9 reshape_reshape.3
  280.3 0.9 copy.88
  281.2 2.2 multiply_reduce_fusion.1
  283.4 1.0 copy.65.lse_ref
  284.4 1.0 copy.66.w_ref
  285.5 1.0 copy.67.y_ref
  286.5 0.7 copy.92
  287.1 0.7 reshape.241.w_ref
  287.9 0.7 reshape.243.y_ref
  288.6 0.7 reshape.239.lse_ref
  289.3 1.3 constant_dynamic-slice_fusion.1
  290.6 1.3 constant_dynamic-slice_fusion
  291.9 1.6 pad_maximum_fusion.z_ref
  293.5 131.9 %table_grad.1 = (f32[3072,960]{1,0:T(8,128)}, f32[1,16384]{1,0:T(1,128)}) custom-call(s32[1]{0:T(128)} %bitcast.15.base_ref, f32[3072,16384]{1,0:T(8,128)} %get-tuple-element.41.lt_ref, bf16[16384,960]{1,0:T(8,128)(2,1)} %get-tuple-element.42.z_ref, f32[1,16384]{1,0:T(1,128)} %reshape.239.lse_ref, f32[1,16384]{1,0:T(1,128)} %reshape.241.w_ref, ...), custom_call_target="tpu_custom_call" | custom-call | flops 96636764160 | bytes 201326592 | tf_op jit(solution)/shard_map/table_grad/pallas_call | solution.py:107
  425.4 0.7 reshape.248.code_ref
  426.1 1.0 copy.68.lse_ref
  427.1 1.0 copy.69.w_ref
  428.1 1.0 copy.70.y_ref
  429.2 1.6 multiply_reduce_fusion
  430.8 0.6 broadcast_in_dim.88
  432.0 29.1 %place_rows.1 = (bf16[1024,1024]{1,0:T(8,128)(2,1)}, bf16[1024,1024]{1,0:T(8,128)(2,1)}) custom-call(s32[16]{0:T(128)} %reduce_sum.161.count_ref, s32[8,2,1024]{2,1,0:T(2,128)} %bitcast.129, bf16[24576,960]{1,0:T(8,128)(2,1)} %all-gather.8.cloned.1.call-done.e_ref), custom_call_target="tpu_custom_call" | custom-call | flops 10000000000 | bytes 47185920 | tf_op jit(solution)/shard_map/place_rows/pallas_call | solution.py:238
  461.1 120.9 %hidden_grad.3 = f32[1024,1024]{1,0:T(8,128)} custom-call(s32[1]{0:T(128)} %bitcast.19.base_ref, bf16[1024,960]{1,0:T(8,128)(2,1)} %pad_maximum_fusion.z_ref, bf16[24576,960]{1,0:T(8,128)(2,1)} %all-gather.8.cloned.1.call-done.e_ref, f32[1024,1]{1,0:T(8,128)} %copy.68.lse_ref, f32[1024,1]{1,0:T(8,128)} %copy.69.w_ref, s32[1024,1]{1,0:T(8,128)} %copy.70.y_ref), custom_call_target="tpu_custom_call" | custom-call | flops 96636764160 | bytes 47185920 | tf_op jit(solution)/shard_map/hidden_grad/pallas_call | solution.py:146
  582.0 2.0 collective-permute-start
  584.1 120.8 %hidden_grad.2 = f32[1024,1024]{1,0:T(8,128)} custom-call(s32[1]{0:T(128)} %bitcast.19.base_ref, bf16[1024,960]{1,0:T(8,128)(2,1)} %copy-done.2, bf16[24576,960]{1,0:T(8,128)(2,1)} %all-gather.8.cloned.1.call-done.e_ref, f32[1024,1]{1,0:T(8,128)} %copy.65.lse_ref, f32[1024,1]{1,0:T(8,128)} %copy.66.w_ref, s32[1024,1]{1,0:T(8,128)} %copy.67.y_ref), custom_call_target="tpu_custom_call" | custom-call | flops 96636764160 | bytes 47185920 | tf_op jit(solution)/shard_map/hidden_grad/pallas_call | solution.py:146
  704.8 36.0 %add_rows.1 = f32[3072,960]{1,0:T(8,128)} custom-call(s32[16]{0:T(128)} %get-tuple-element.49.count_ref, s32[16,1,1024]{2,1,0:T(1,128)} %reshape.248.code_ref, bf16[16384,960]{1,0:T(8,128)(2,1)} %bitcast.119, f32[3072,960]{1,0:T(8,128)} %get-tuple-element.51.grad_ref), custom_call_target="tpu_custom_call" | custom-call | flops 10000000000 | bytes 31457280 | tf_op jit(solution)/shard_map/add_rows/pallas_call | solution.py:184
  740.8 12.3 %copy.74 = f32[3072,960]{0,1:T(8,128)} copy(f32[3072,960]{1,0:T(8,128)} %add_rows.1) | data formatting | bytes 23592960
  753.1 1.3 copy-done.3
  754.4 4.0 fusion.15
  758.4 3.9 copy.72
  762.4 5.8 fusion.11
  768.3 0.7 maximum_maximum_fusion
  769.0 7.0 exchange.7
  776.0 0.7 reduce_sum.168
  777.9 3.4 fusion.31
  781.6 2.4 copy.73
  (84 shorter events, 8.2 us)
Async XLA Ops:
  7.2 100.6 %all-gather.6.cloned.1.call-start = ((), (), s32[]{:S(2)}) async-start(), calls=%async_computation | async-start | bytes 17825792 | tf_op jit(solution)/shard_map/all_gather | solution.py:351
  25.9 2.7 copy-start
  26.3 4.0 copy-start.7
  27.0 0.6 copy-start.13
  27.1 3.2 copy-start.11
  27.7 2.6 copy-start.9
  28.7 2.0 copy-start.2
  30.7 155.9 %all-gather.10.cloned.1.call-start = ((), (), s32[]{:S(2)}) async-start(), calls=%async_computation.2 | async-start | bytes 17825792 | tf_op jit(solution)/shard_map/all_gather | solution.py:351
  31.4 400.5 %all-gather.8.cloned.1.call-start = ((), (), s32[]{:S(2)}) async-start(), calls=%async_computation.1 | async-start | bytes 56623104 | tf_op jit(solution)/shard_map/all_gather | solution.py:380
  40.0 1.5 copy-start.4
  40.0 664.8 %all-gather.12.cloned.1.call-start = ((), (), s32[]{:S(2)}) async-start(), calls=%async_computation.3 | async-start | bytes 35651584 | tf_op jit(solution)/shard_map/all_gather | solution.py:395
  186.6 71.3 %copy-start.16 = (f32[1,8192]{1,0:T(1,128)S(1)}, f32[1,8192]{1,0:T(1,128)}, u32[]{:S(2)}) copy-start(f32[1,8192]{1,0:T(1,128)} %get-tuple-element.35) | copy-start | bytes 98308
  186.6 72.2 %copy-start.15 = (f32[1,8192]{1,0:T(1,128)S(1)}, f32[1,8192]{1,0:T(1,128)}, u32[]{:S(2)}) copy-start(f32[1,8192]{1,0:T(1,128)} %get-tuple-element.39) | copy-start | bytes 98308
  293.5 131.9 %copy-start.5 = (s32[16,1024]{1,0:T(8,128)S(1)}, s32[16,1024]{1,0:T(8,128)}, u32[]{:S(2)}) copy-start(s32[16,1024]{1,0:T(8,128)} %select_reduce_fusion.1) | copy-start | bytes 196612
  293.5 135.7 %copy-start.6 = (f32[1,16384]{1,0:T(1,128)S(1)}, f32[1,16384]{1,0:T(1,128)}, u32[]{:S(2)}) copy-start(f32[1,16384]{1,0:T(1,128)} %reshape.241.w_ref) | copy-start | bytes 196612
  582.0 180.3 %collective-permute-start.1 = (f32[1024,1024]{1,0:T(8,128)}, f32[1024,1024]{1,0:T(8,128)}, u32[]{:S(2)}, u32[]{:S(2)}) collective-permute-start(f32[1024,1024]{1,0:T(8,128)} %hidden_grad.3), channel_id=1, source_target_pairs={{0,8},{1,9},{2,10},{3,11},{4,12},{5,13},{6,14},{7,15},{8,0},{9,1},... | collective-permute-start | bytes 12582920 | tf_op jit(solution)/shard_map/ppermute | solution.py:388
  582.0 171.0 %collective-permute-start = (bf16[1024,1024]{1,0:T(8,128)(2,1)}, bf16[1024,1024]{1,0:T(8,128)(2,1)S(1)}, u32[]{:S(2)}, u32[]{:S(2)}) collective-permute-start(bf16[1024,1024]{1,0:T(8,128)(2,1)} %get-tuple-element.33), channel_id=1, source_target_pairs={{0,8},{1,9},{2,10},{3,11},{4,12},{5,13},{6,14},{7,15},{8,0},{9,1},... | collective-permute-start | bytes 6291464 | tf_op jit(solution)/shard_map/ppermute | solution.py:391
  740.8 13.6 %copy-start.17 = (pred[1024]{0:T(1024)(128)(4,1)S(1)}, pred[1024]{0:T(1024)(128)(4,1)}, u32[]{:S(2)}) copy-start(pred[1024]{0:T(1024)(128)(4,1)} %fusion.28) | copy-start | bytes 3076
  753.1 1.3 copy-start.3
  754.4 8.0 %copy-start.1 = (bf16[1,1024,960]{2,1,0:T(8,128)(2,1)S(1)}, bf16[1,1024,960]{2,1,0:T(8,128)(2,1)}, u32[]{:S(2)}) copy-start(bf16[1,1024,960]{2,1,0:T(8,128)(2,1)} %copy-done) | copy-start | bytes 5898244
  754.4 8.0 %copy-start.8 = (f32[1024]{0:T(1024)S(1)}, f32[1024]{0:T(1024)}, u32[]{:S(2)}) copy-start(f32[1024]{0:T(1024)} %copy-done.7) | copy-start | bytes 12292
  754.4 8.0 %copy-start.10 = (f32[960]{0:T(1024)S(1)}, f32[960]{0:T(1024)}, u32[]{:S(2)}) copy-start(f32[960]{0:T(1024)} %copy-done.9) | copy-start | bytes 11524
  754.4 8.0 %copy-start.12 = (f32[1024]{0:T(1024)S(1)}, f32[1024]{0:T(1024)}, u32[]{:S(2)}) copy-start(f32[1024]{0:T(1024)} %copy-done.11) | copy-start | bytes 12292
  762.3 6.0 copy-start.18
  769.0 8.9 %copy-start.14 = (f32[1024]{0:T(1024)S(1)}, f32[1024]{0:T(1024)}, u32[]{:S(2)}) copy-start(f32[1024]{0:T(1024)} %copy-done.13) | copy-start | bytes 12292
Sparse Core Ops, SparseCore 0:
  30.8 76.8 all-gather.5
  110.5 76.0 all-gather.9
  189.1 229.8 all-gather.7
  421.0 131.2 all-gather.11

commit v4 on v3

--- a/solution.py
+++ b/solution.py
@@ -100,7 +100,7 @@
     ll_ref[...] = label_logit
 
 
-def table_grad(base, lt, z, lse, w, y, pt=1024, sub=256):
+def table_grad(base, lt, z, lse, w, y, pt=1024, sub=512):
     n_v, n_p = lt.shape
     dim = z.shape[1]
     row = pl.BlockSpec((1, pt), lambda i, b: (0, i))
@@ -138,11 +138,11 @@
         acc_ref[rows, :e.shape[1]] += jnp.dot(d, e, preferred_element_type=F32)
 
 
-def hidden_grad(base, z, e, lse, w, y, tp=512, tv=768):
+def hidden_grad(base, which, z, e, lse, w, y, tp=512, tv=768):
     n_v, dim = e.shape
     n_p = z.shape[0]
     wide = pl.cdiv(dim, 128) * 128
-    col = pl.BlockSpec((n_p, 1), lambda i, b: (0, 0))
+    col = pl.BlockSpec((n_p, 1), lambda i, b: (which, 0))
     return pl.pallas_call(
         functools.partial(hidden_grad_body, tp=tp, n_tp=n_p // tp, tv=tv),
         grid_spec=pltpu.PrefetchScalarGridSpec(
@@ -163,7 +163,7 @@
 
     @pl.when(b == 0)
     def _():
-        acc_ref[...] = grad_ref[...]
+        pltpu.sync_copy(grad_ref, acc_ref)
 
     rows_ref[...] = de_ref[...].astype(F32)
 
@@ -189,7 +189,7 @@
             in_specs=[
                 pl.BlockSpec((1, 1, n_p), lambda b, c: (b, 0, 0), memory_space=pltpu.SMEM),
                 pl.BlockSpec((n_p, dim), lambda b, c: (b, 0)),
-                pl.BlockSpec((n_v, dim), whole, pipeline_mode=pl.Buffered(1)),
+                pl.BlockSpec(memory_space=pl.ANY),
             ],
             out_specs=pl.BlockSpec((n_v, dim), whole, pipeline_mode=pl.Buffered(1)),
             scratch_shapes=[pltpu.VMEM((n_p, dim), F32)],
@@ -345,12 +345,21 @@
         look_codes, look_counts = pack(look.reshape(2 * half, seq))
         in_half = (tok_own // (half * n_v)) == plane
 
+        def by_chunk(a):
+            return a.reshape(n_dev, CHUNKS, part).transpose(1, 0, 2).reshape(1, total)
+
+        def columns(a):
+            return jnp.concatenate([row_of(a, other), row_of(a, me)])[:, None]
+
+        early = (codes, counts, look_codes, look_counts, by_chunk(weight_all), by_chunk(label_all), columns(weight_all), columns(label_all))
+
         carry = None
         maxes, sums, z_parts = [], [], []
         for c in range(CHUNKS):
             z_c = lax.all_gather(z[c * part:(c + 1) * part], 'fsdp', axis=0, tiled=True)
             if c == 0:
-                z_c, codes, counts, look_codes, look_counts = lax.optimization_barrier((z_c, codes, counts, look_codes, look_counts))
+                z_c, early = lax.optimization_barrier((z_c, early))
+                codes, counts, look_codes, look_counts, w_row, y_row, w_col, y_col = early
             lt, z_all, m_c, s_c = logits_pass(table_shard, z_c, carry, c, total)
             carry = (lt, z_all)
             maxes.append(m_c)
@@ -368,28 +377,26 @@
         row_sum = jnp.sum(pair_sum * jnp.exp(pair_max - row_max[None]), axis=0)
         lse_all = exchange((row_max + jnp.log(row_sum))[None], n_dev, False, 3).reshape(n_dev, seq)
 
-        def by_chunk(a):
-            return a.reshape(n_dev, CHUNKS, part).transpose(1, 0, 2).reshape(1, total)
-
         base = (me * n_v).astype(jnp.int32).reshape(1)
-        w_row = by_chunk(weight_all)
-        d_table, label_logit = table_grad(base, lt, z_all, by_chunk(lse_all), w_row, by_chunk(label_all))
+        d_table, label_logit = table_grad(base, lt, z_all, by_chunk(lse_all), w_row, y_row)
         loss_lse = jnp.sum(weight_all * lse_all)
         loss_hit = jnp.sum(w_row * label_logit)
 
         e_half = lax.all_gather(table_shard, 'fsdp', axis=0, tiled=True, axis_index_groups=planes)
         half_base = (plane * half * n_v).astype(jnp.int32)
 
-        def half_grad(d, z_d):
-            return hidden_grad(half_base.reshape(1), z_d, e_half, row_of(lse_all, d)[:, None], row_of(weight_all, d)[:, None], row_of(label_all, d)[:, None])
+        cols = columns(lse_all), w_col, y_col
+
+        def half_grad(which, z_d):
+            return hidden_grad(half_base.reshape(1), which, z_d, e_half, *cols)
 
         z_other, d_table = lax.optimization_barrier((z_other, d_table))
-        dz_other = half_grad(other, z_other)
+        dz_other = half_grad(0, z_other)
         dz_other = lax.ppermute(dz_other, 'fsdp', partner)
         found_other, found_own = place_rows(look_counts, look_codes.reshape(2, half, seq), e_half)
         found_other, z = lax.optimization_barrier((found_other, z))
         found_other = lax.ppermute(found_other, 'fsdp', partner)
-        dz_own = half_grad(me, z)
+        dz_own = half_grad(1, z)
         emb_rows = jnp.where(in_half[:, None], found_own[:, :dim], found_other[:, :dim]).reshape(1, seq, dim)
 
         de_all = lax.all_gather(d_emb.reshape(seq, dim), 'fsdp', axis=0, tiled=True)

time: 798 us -> 797 us (level)
    unnamed x46 -> x52, local copies, waits for them, and re-layouts: 37.6 us -> 37.5 us
  transfers between devices with their start and end apart: 6 -> 6, of which waited for: 2 -> 2; matrix products, arithmetic and copies ran while one was open for 10% -> 10% of each run, Pallas kernels for 75% -> 76%
where the time goes in v4:
time: 797 us; the launch traced here: 792 us
  Pallas kernels  620 us (78%)
  local copies, waits for them, and re-layouts  55.1 us (7%)
  other arithmetic  48.4 us (6%)
  waiting for transfers between devices  48.2 us (6%)
  between operations  16.8 us (2%)
    pallas_call x2, Pallas kernels, hidden_grad(): pl.pallas_call(functools.partial(hidden_grad_body, tp=tp, n_tp=n_p // tp,...  242 us
    pallas_call x2, Pallas kernels, logits_pass(): pl.pallas_call(functools.partial(logits_body, sub=sub, n_sub=n_v // sub),...  142 us
    pallas_call x1, Pallas kernels, table_grad(): pl.pallas_call(functools.partial(table_grad_body, sub=sub, n_sub=n_v // s...  135 us
    all_gather x2, waiting for transfers between devices, device_step(): z_c = lax.all_gather(z[c * part:(c + 1) * part], 'fsdp', axis=0, tiled=True)  47.4 us
    unnamed x52, local copies, waits for them, and re-layouts  37.5 us
    pallas_call x1, Pallas kernels, add_rows(): pl.pallas_call(add_rows_body, grid_spec=pltpu.PrefetchScalarGridSpec(num_...  36.3 us
    pallas_call x4, Pallas kernels, exchange(): pl.pallas_call(functools.partial(exchange_body, axis=axis, n_dev=n_dev, s...  35.1 us
    pallas_call x1, Pallas kernels, place_rows(): pl.pallas_call(place_rows_body, grid_spec=pltpu.PrefetchScalarGridSpec(nu...  29.2 us
  transfers between devices with their start and end apart: 6, of which 2 were waited for; matrix products, arithmetic and copies ran while one was open for 10% of the time, Pallas kernels for 76%

profile of v4, /device:TPU:0, one launch (start us, length us, event | category | flops | bytes accessed | tf_op | source)
XLA Modules:
  0.0 791.7 jit_solution(187682159650433324)
XLA Ops:
  7.2 0.7 convert_element_type.54
  7.9 0.7 convert_element_type.56
  8.6 0.7 convert_element_type.58
  9.3 0.7 concatenate.21
  10.0 0.6 pad_bitcast_fusion.x_ref
  10.6 11.3 %exchange.4 = f32[16,32,128]{2,1,0:T(8,128)} custom-call(f32[1,32,128]{2,1,0:T(8,128)} %pad_bitcast_fusion.x_ref), custom_call_target="tpu_custom_call" | custom-call | flops 4000000000 | tf_op jit(solution)/shard_map/exchange/pallas_call | solution.py:283
  22.0 1.1 copy.87
  23.1 2.8 copy.53
  26.3 0.7 fusion.10
  27.8 0.8 fusion.8.z_ref
  28.7 1.6 fusion.32
  30.7 0.7 all-gather.10.cloned.1.call-update
  31.4 8.5 %copy.57.refs_0_ = bf16[3072,960]{1,0:T(8,128)(2,1)} copy(bf16[3072,960]{0,1:T(8,128)(2,1)} %param.13) | data formatting | bytes 11796480 | tf_op args[5]
  40.6 0.9 copy-done.4
  41.5 2.5 copy.71
  44.2 0.6 slice_reduce_fusion
  44.8 0.7 slice_convert_fusion
  46.4 0.7 reshape.228.w_ref
  47.1 0.7 reshape.230.y_ref
  48.8 0.7 convert_reduce_fusion.2
  49.9 8.8 %select_reduce_fusion = s32[16,1024]{1,0:T(8,128)S(1)} fusion(s32[16,1024]{1,0:T(8,128)S(1)} %get-tuple-element.102, s32[16,1024]{1,0:T(8,128)S(1)} %fusion.21), kind=kLoop, calls=%fused_computation | loop fusion | flops 50315264 | bytes 196608 | tf_op jit(solution)/shard_map/reduce_sum | solution.py:338
  58.7 9.4 %select_reduce_fusion.1 = s32[16,1024]{1,0:T(8,128)} fusion(s32[16,1024]{1,0:T(8,128)S(1)} %get-tuple-element.103, s32[16,1024]{1,0:T(8,128)S(1)} %fusion.18), kind=kLoop, calls=%fused_computation.2 | loop fusion | flops 50315264 | bytes 196608 | tf_op jit(solution)/shard_map/reduce_sum | solution.py:338
  68.1 39.5 %all-gather.6.cloned.1.call-done.refs_1_ = bf16[8192,960]{1,0:T(8,128)(2,1)} async-done(((bf16[512,960]{1,0:T(8,128)(2,1)}), bf16[8192,960]{1,0:T(8,128)(2,1)}) %all-gather.6.cloned.1.call-update) | async-done | bytes 15728656 | tf_op jit(solution)/shard_map/all_gather | solution.py:359
  107.6 71.0 %logits_pass.2 = (f32[3072,16384]{1,0:T(8,128)}, bf16[16384,960]{1,0:T(8,128)(2,1)}, f32[1,8192]{1,0:T(1,128)}, f32[1,8192]{1,0:T(1,128)}) custom-call(bf16[3072,960]{1,0:T(8,128)(2,1)} %copy.57.refs_0_, bf16[8192,960]{1,0:T(8,128)(2,1)} %all-gather.6.cloned.1.call-done.refs_1_), custom_call_target="tpu_custom_call" | custom-call | flops 48318382080 | bytes 106561536 | tf_op jit(solution)/shard_map/logits_pass/pallas_call | solution.py:58
  178.6 7.9 all-gather.10.cloned.1.call-done.refs_1_
  186.6 71.3 %logits_pass.3 = (f32[3072,16384]{1,0:T(8,128)}, bf16[16384,960]{1,0:T(8,128)(2,1)}, f32[1,8192]{1,0:T(1,128)}, f32[1,8192]{1,0:T(1,128)}) custom-call(bf16[3072,960]{1,0:T(8,128)(2,1)} %copy.57.refs_0_, bf16[8192,960]{1,0:T(8,128)(2,1)} %all-gather.10.cloned.1.call-done.refs_1_, ...), custom_call_target="tpu_custom_call", output_to_operand_aliasing={{0}: (2, {}), {1}: (3, {})} | custom-call | flops 48318382080 | bytes 106561536 | tf_op jit(solution)/shard_map/logits_pass/pallas_call | solution.py:58
  257.8 0.8 pad_maximum_fusion.2
  258.7 0.8 pad_maximum_fusion.3
  259.6 0.7 pad_maximum_fusion.1.x_ref
  260.3 9.0 %exchange.5 = f32[16,16,128]{2,1,0:T(8,128)} custom-call(f32[16,16,128]{2,1,0:T(8,128)} %pad_maximum_fusion.1.x_ref), custom_call_target="tpu_custom_call" | custom-call | flops 4000000000 | tf_op jit(solution)/shard_map/exchange/pallas_call | solution.py:283
  269.3 0.9 slice_reduce_fusion.1
  270.2 0.9 multiply_reduce_fusion.2
  271.1 0.6 add_bitcast_fusion.x_ref
  271.7 7.8 exchange.6
  279.4 0.9 reshape_reshape.3
  280.3 0.9 copy.88
  281.2 1.3 copy.65.lse_ref
  282.5 0.7 copy.92
  283.2 1.3 copy.66.w_ref
  284.6 1.4 copy.67.y_ref
  285.9 0.7 reshape.237.lse_ref
  286.6 1.3 constant_dynamic-slice_fusion.3
  287.9 1.3 constant_dynamic-slice_fusion.2
  289.2 1.6 pad_maximum_fusion.z_ref
  290.9 135.2 %table_grad.1 = (f32[3072,960]{1,0:T(8,128)}, f32[1,16384]{1,0:T(1,128)}) custom-call(s32[1]{0:T(128)} %bitcast.23.base_ref, f32[3072,16384]{1,0:T(8,128)} %get-tuple-element.45.lt_ref, bf16[16384,960]{1,0:T(8,128)(2,1)} %get-tuple-element.46.z_ref, f32[1,16384]{1,0:T(1,128)} %reshape.237.lse_ref, f32[1,16384]{1,0:T(1,128)} %reshape.228.w_ref, ...), custom_call_target="tpu_custom_call" | custom-call | flops 96636764160 | bytes 201326592 | tf_op jit(solution)/shard_map/table_grad/pallas_call | solution.py:107
  426.0 0.7 reshape.242.code_ref
  426.7 1.6 multiply_reduce_fusion
  428.3 0.6 broadcast_in_dim.76
  429.5 0.6 multiply_reduce_fusion.1
  430.2 29.2 %place_rows.1 = (bf16[1024,1024]{1,0:T(8,128)(2,1)}, bf16[1024,1024]{1,0:T(8,128)(2,1)}) custom-call(s32[16]{0:T(128)} %reduce_sum.161.count_ref, s32[8,2,1024]{2,1,0:T(2,128)} %bitcast.126, bf16[24576,960]{1,0:T(8,128)(2,1)} %all-gather.8.cloned.1.call-done.e_ref), custom_call_target="tpu_custom_call" | custom-call | flops 10000000000 | bytes 47185920 | tf_op jit(solution)/shard_map/place_rows/pallas_call | solution.py:238
  459.3 121.1 %hidden_grad.3 = f32[1024,1024]{1,0:T(8,128)} custom-call(s32[1]{0:T(128)} %bitcast.25.base_ref, bf16[1024,960]{1,0:T(8,128)(2,1)} %pad_maximum_fusion.z_ref, bf16[24576,960]{1,0:T(8,128)(2,1)} %all-gather.8.cloned.1.call-done.e_ref, f32[2048,1]{1,0:T(8,128)} %copy.65.lse_ref, f32[2048,1]{1,0:T(8,128)} %copy.66.w_ref, s32[2048,1]{1,0:T(8,128)} %copy.67.y_ref), custom_call_target="tpu_custom_call" | custom-call | flops 96636764160 | bytes 47185920 | tf_op jit(solution)/shard_map/hidden_grad/pallas_call | solution.py:146
  580.4 2.0 collective-permute-start
  582.4 120.7 %hidden_grad.2 = f32[1024,1024]{1,0:T(8,128)} custom-call(s32[1]{0:T(128)} %bitcast.25.base_ref, bf16[1024,960]{1,0:T(8,128)(2,1)} %copy-done.2, bf16[24576,960]{1,0:T(8,128)(2,1)} %all-gather.8.cloned.1.call-done.e_ref, f32[2048,1]{1,0:T(8,128)} %copy.65.lse_ref, f32[2048,1]{1,0:T(8,128)} %copy.66.w_ref, s32[2048,1]{1,0:T(8,128)} %copy.67.y_ref), custom_call_target="tpu_custom_call" | custom-call | flops 96636764160 | bytes 47185920 | tf_op jit(solution)/shard_map/hidden_grad/pallas_call | solution.py:146
  703.2 36.3 %add_rows.1 = f32[3072,960]{1,0:T(8,128)} custom-call(s32[16]{0:T(128)} %get-tuple-element.57.count_ref, s32[16,1,1024]{2,1,0:T(1,128)} %reshape.242.code_ref, bf16[16384,960]{1,0:T(8,128)(2,1)} %bitcast.116, f32[3072,960]{1,0:T(8,128)} %get-tuple-element.59.grad_ref), custom_call_target="tpu_custom_call" | custom-call | flops 10000000000 | bytes 31457280 | tf_op jit(solution)/shard_map/add_rows/pallas_call | solution.py:184
  739.4 12.3 %copy.74 = f32[3072,960]{0,1:T(8,128)} copy(f32[3072,960]{1,0:T(8,128)} %add_rows.1) | data formatting | bytes 23592960
  751.7 1.3 copy-done.3
  753.0 4.0 fusion.15
  757.0 3.9 copy.72
  761.0 5.8 fusion.11
  766.9 0.7 maximum_maximum_fusion
  767.6 7.0 exchange.7
  774.6 0.7 reduce_sum.168
  776.5 3.4 fusion.31
  780.2 2.4 copy.73
  (91 shorter events, 7.0 us)
Async XLA Ops:
  7.2 100.5 %all-gather.6.cloned.1.call-start = ((), (), s32[]{:S(2)}) async-start(), calls=%async_computation | async-start | bytes 17825792 | tf_op jit(solution)/shard_map/all_gather | solution.py:359
  25.9 2.7 copy-start
  26.3 4.0 copy-start.10
  27.0 0.6 copy-start.16
  27.1 3.2 copy-start.14
  27.7 2.6 copy-start.12
  28.7 2.0 copy-start.2
  30.6 155.9 %all-gather.10.cloned.1.call-start = ((), (), s32[]{:S(2)}) async-start(), calls=%async_computation.2 | async-start | bytes 17825792 | tf_op jit(solution)/shard_map/all_gather | solution.py:359
  31.4 398.8 %all-gather.8.cloned.1.call-start = ((), (), s32[]{:S(2)}) async-start(), calls=%async_computation.1 | async-start | bytes 56623104 | tf_op jit(solution)/shard_map/all_gather | solution.py:385
  40.0 1.5 copy-start.4
  40.0 663.2 %all-gather.12.cloned.1.call-start = ((), (), s32[]{:S(2)}) async-start(), calls=%async_computation.3 | async-start | bytes 35651584 | tf_op jit(solution)/shard_map/all_gather | solution.py:402
  45.5 133.2 %copy-start.5 = (f32[16,1024]{1,0:T(8,128)}, f32[16,1024]{1,0:T(8,128)S(1)}, u32[]{:S(2)}) copy-start(f32[16,1024]{1,0:T(8,128)S(1)} %get-tuple-element.91) | copy-start | bytes 196612
  186.6 71.3 %copy-start.19 = (f32[1,8192]{1,0:T(1,128)S(1)}, f32[1,8192]{1,0:T(1,128)}, u32[]{:S(2)}) copy-start(f32[1,8192]{1,0:T(1,128)} %get-tuple-element.39) | copy-start | bytes 98308
  186.6 72.2 %copy-start.18 = (f32[1,8192]{1,0:T(1,128)S(1)}, f32[1,8192]{1,0:T(1,128)}, u32[]{:S(2)}) copy-start(f32[1,8192]{1,0:T(1,128)} %get-tuple-element.43) | copy-start | bytes 98308
  290.9 135.2 %copy-start.8 = (s32[16,1024]{1,0:T(8,128)S(1)}, s32[16,1024]{1,0:T(8,128)}, u32[]{:S(2)}) copy-start(s32[16,1024]{1,0:T(8,128)} %select_reduce_fusion.1) | copy-start | bytes 196612
  290.9 135.9 %copy-start.9 = (f32[1,16384]{1,0:T(1,128)S(1)}, f32[1,16384]{1,0:T(1,128)}, u32[]{:S(2)}) copy-start(f32[1,16384]{1,0:T(1,128)} %reshape.228.w_ref) | copy-start | bytes 196612
  290.9 138.7 %copy-start.6 = (f32[16,1024]{1,0:T(8,128)S(1)}, f32[16,1024]{1,0:T(8,128)}, u32[]{:S(2)}) copy-start(f32[16,1024]{1,0:T(8,128)} %copy-done.5) | copy-start | bytes 196612
  290.9 138.7 %copy-start.7 = (f32[16,8,128]{2,1,0:T(8,128)S(1)}, f32[16,8,128]{2,1,0:T(8,128)}, u32[]{:S(2)}) copy-start(f32[16,8,128]{2,1,0:T(8,128)} %exchange.6) | copy-start | bytes 196612
  580.4 180.5 %collective-permute-start.1 = (f32[1024,1024]{1,0:T(8,128)}, f32[1024,1024]{1,0:T(8,128)}, u32[]{:S(2)}, u32[]{:S(2)}) collective-permute-start(f32[1024,1024]{1,0:T(8,128)} %hidden_grad.3), channel_id=1, source_target_pairs={{0,8},{1,9},{2,10},{3,11},{4,12},{5,13},{6,14},{7,15},{8,0},{9,1},... | collective-permute-start | bytes 12582920 | tf_op jit(solution)/shard_map/ppermute | solution.py:395
  580.4 171.3 %collective-permute-start = (bf16[1024,1024]{1,0:T(8,128)(2,1)}, bf16[1024,1024]{1,0:T(8,128)(2,1)S(1)}, u32[]{:S(2)}, u32[]{:S(2)}) collective-permute-start(bf16[1024,1024]{1,0:T(8,128)(2,1)} %get-tuple-element.37), channel_id=1, source_target_pairs={{0,8},{1,9},{2,10},{3,11},{4,12},{5,13},{6,14},{7,15},{8,0},{9,1},... | collective-permute-start | bytes 6291464 | tf_op jit(solution)/shard_map/ppermute | solution.py:398
  739.4 13.6 %copy-start.20 = (pred[1024]{0:T(1024)(128)(4,1)S(1)}, pred[1024]{0:T(1024)(128)(4,1)}, u32[]{:S(2)}) copy-start(pred[1024]{0:T(1024)(128)(4,1)} %fusion.28) | copy-start | bytes 3076
  751.7 1.3 copy-start.3
  753.0 7.9 %copy-start.1 = (bf16[1,1024,960]{2,1,0:T(8,128)(2,1)S(1)}, bf16[1,1024,960]{2,1,0:T(8,128)(2,1)}, u32[]{:S(2)}) copy-start(bf16[1,1024,960]{2,1,0:T(8,128)(2,1)} %copy-done) | copy-start | bytes 5898244
  753.0 8.0 %copy-start.11 = (f32[1024]{0:T(1024)S(1)}, f32[1024]{0:T(1024)}, u32[]{:S(2)}) copy-start(f32[1024]{0:T(1024)} %copy-done.10) | copy-start | bytes 12292
  753.0 8.0 %copy-start.13 = (f32[960]{0:T(1024)S(1)}, f32[960]{0:T(1024)}, u32[]{:S(2)}) copy-start(f32[960]{0:T(1024)} %copy-done.12) | copy-start | bytes 11524
  753.0 8.0 %copy-start.15 = (f32[1024]{0:T(1024)S(1)}, f32[1024]{0:T(1024)}, u32[]{:S(2)}) copy-start(f32[1024]{0:T(1024)} %copy-done.14) | copy-start | bytes 12292
  760.9 6.0 copy-start.21
  767.6 8.9 %copy-start.17 = (f32[1024]{0:T(1024)S(1)}, f32[1024]{0:T(1024)}, u32[]{:S(2)}) copy-start(f32[1024]{0:T(1024)} %copy-done.16) | copy-start | bytes 12292
Sparse Core Ops, SparseCore 0:
  30.8 76.8 all-gather.5
  110.5 76.0 all-gather.9
  189.0 229.8 all-gather.7
  421.0 131.2 all-gather.11

commit v5 on v4

--- a/solution.py
+++ b/solution.py
@@ -100,7 +100,7 @@
     ll_ref[...] = label_logit
 
 
-def table_grad(base, lt, z, lse, w, y, pt=1024, sub=512):
+def table_grad(base, lt, z, lse, w, y, pt=1024, sub=256):
     n_v, n_p = lt.shape
     dim = z.shape[1]
     row = pl.BlockSpec((1, pt), lambda i, b: (0, i))

time: 797 us -> 793 us (level)
  no operation moved by 1% of the time
where the time goes in v5:
time: 793 us; the launch traced here: 788 us
  Pallas kernels  617 us (78%)
  local copies, waits for them, and re-layouts  55.1 us (7%)
  other arithmetic  48.4 us (6%)
  waiting for transfers between devices  48.2 us (6%)
  between operations  16.8 us (2%)
    pallas_call x2, Pallas kernels, hidden_grad(): pl.pallas_call(functools.partial(hidden_grad_body, tp=tp, n_tp=n_p // tp,...  242 us
    pallas_call x2, Pallas kernels, logits_pass(): pl.pallas_call(functools.partial(logits_body, sub=sub, n_sub=n_v // sub),...  142 us
    pallas_call x1, Pallas kernels, table_grad(): pl.pallas_call(functools.partial(table_grad_body, sub=sub, n_sub=n_v // s...  132 us
    all_gather x2, waiting for transfers between devices, device_step(): z_c = lax.all_gather(z[c * part:(c + 1) * part], 'fsdp', axis=0, tiled=True)  47.4 us
    unnamed x52, local copies, waits for them, and re-layouts  37.5 us
    pallas_call x1, Pallas kernels, add_rows(): pl.pallas_call(add_rows_body, grid_spec=pltpu.PrefetchScalarGridSpec(num_...  36.2 us
    pallas_call x4, Pallas kernels, exchange(): pl.pallas_call(functools.partial(exchange_body, axis=axis, n_dev=n_dev, s...  35.1 us
    pallas_call x1, Pallas kernels, place_rows(): pl.pallas_call(place_rows_body, grid_spec=pltpu.PrefetchScalarGridSpec(nu...  29.3 us
  transfers between devices with their start and end apart: 6, of which 2 were waited for; matrix products, arithmetic and copies ran while one was open for 10% of the time, Pallas kernels for 76%

profile of v5, /device:TPU:0, one launch (start us, length us, event | category | flops | bytes accessed | tf_op | source)
XLA Modules:
  0.0 788.4 jit_solution(16859232712567097493)
XLA Ops:
  7.2 0.7 convert_element_type.54
  7.9 0.7 convert_element_type.56
  8.6 0.7 convert_element_type.58
  9.3 0.7 concatenate.21
  10.0 0.6 pad_bitcast_fusion.x_ref
  10.6 11.3 %exchange.4 = f32[16,32,128]{2,1,0:T(8,128)} custom-call(f32[1,32,128]{2,1,0:T(8,128)} %pad_bitcast_fusion.x_ref), custom_call_target="tpu_custom_call" | custom-call | flops 4000000000 | tf_op jit(solution)/shard_map/exchange/pallas_call | solution.py:283
  22.0 1.1 copy.87
  23.1 2.8 copy.53
  26.3 0.7 fusion.10
  27.8 0.8 fusion.8.z_ref
  28.7 1.6 fusion.32
  30.7 0.7 all-gather.10.cloned.1.call-update
  31.4 8.5 %copy.57.refs_0_ = bf16[3072,960]{1,0:T(8,128)(2,1)} copy(bf16[3072,960]{0,1:T(8,128)(2,1)} %param.13) | data formatting | bytes 11796480 | tf_op args[5]
  40.6 0.9 copy-done.4
  41.5 2.5 copy.71
  44.2 0.6 slice_reduce_fusion
  44.8 0.7 slice_convert_fusion
  46.4 0.7 reshape.228.w_ref
  47.1 0.7 reshape.230.y_ref
  48.8 0.7 convert_reduce_fusion.2
  49.9 8.8 %select_reduce_fusion = s32[16,1024]{1,0:T(8,128)S(1)} fusion(s32[16,1024]{1,0:T(8,128)S(1)} %get-tuple-element.102, s32[16,1024]{1,0:T(8,128)S(1)} %fusion.21), kind=kLoop, calls=%fused_computation | loop fusion | flops 50315264 | bytes 196608 | tf_op jit(solution)/shard_map/reduce_sum | solution.py:338
  58.7 9.4 %select_reduce_fusion.1 = s32[16,1024]{1,0:T(8,128)} fusion(s32[16,1024]{1,0:T(8,128)S(1)} %get-tuple-element.103, s32[16,1024]{1,0:T(8,128)S(1)} %fusion.18), kind=kLoop, calls=%fused_computation.2 | loop fusion | flops 50315264 | bytes 196608 | tf_op jit(solution)/shard_map/reduce_sum | solution.py:338
  68.1 39.5 %all-gather.6.cloned.1.call-done.refs_1_ = bf16[8192,960]{1,0:T(8,128)(2,1)} async-done(((bf16[512,960]{1,0:T(8,128)(2,1)}), bf16[8192,960]{1,0:T(8,128)(2,1)}) %all-gather.6.cloned.1.call-update) | async-done | bytes 15728656 | tf_op jit(solution)/shard_map/all_gather | solution.py:359
  107.6 71.0 %logits_pass.2 = (f32[3072,16384]{1,0:T(8,128)}, bf16[16384,960]{1,0:T(8,128)(2,1)}, f32[1,8192]{1,0:T(1,128)}, f32[1,8192]{1,0:T(1,128)}) custom-call(bf16[3072,960]{1,0:T(8,128)(2,1)} %copy.57.refs_0_, bf16[8192,960]{1,0:T(8,128)(2,1)} %all-gather.6.cloned.1.call-done.refs_1_), custom_call_target="tpu_custom_call" | custom-call | flops 48318382080 | bytes 106561536 | tf_op jit(solution)/shard_map/logits_pass/pallas_call | solution.py:58
  178.6 7.9 %all-gather.10.cloned.1.call-done.refs_1_ = bf16[8192,960]{1,0:T(8,128)(2,1)} async-done(((bf16[512,960]{1,0:T(8,128)(2,1)}), bf16[8192,960]{1,0:T(8,128)(2,1)}) %all-gather.10.cloned.1.call-update) | async-done | bytes 15728656 | tf_op jit(solution)/shard_map/all_gather | solution.py:359
  186.6 71.3 %logits_pass.3 = (f32[3072,16384]{1,0:T(8,128)}, bf16[16384,960]{1,0:T(8,128)(2,1)}, f32[1,8192]{1,0:T(1,128)}, f32[1,8192]{1,0:T(1,128)}) custom-call(bf16[3072,960]{1,0:T(8,128)(2,1)} %copy.57.refs_0_, bf16[8192,960]{1,0:T(8,128)(2,1)} %all-gather.10.cloned.1.call-done.refs_1_, ...), custom_call_target="tpu_custom_call", output_to_operand_aliasing={{0}: (2, {}), {1}: (3, {})} | custom-call | flops 48318382080 | bytes 106561536 | tf_op jit(solution)/shard_map/logits_pass/pallas_call | solution.py:58
  257.8 0.8 pad_maximum_fusion.2
  258.7 0.8 pad_maximum_fusion.3
  259.6 0.7 pad_maximum_fusion.1.x_ref
  260.3 9.0 %exchange.5 = f32[16,16,128]{2,1,0:T(8,128)} custom-call(f32[16,16,128]{2,1,0:T(8,128)} %pad_maximum_fusion.1.x_ref), custom_call_target="tpu_custom_call" | custom-call | flops 4000000000 | tf_op jit(solution)/shard_map/exchange/pallas_call | solution.py:283
  269.3 0.9 slice_reduce_fusion.1
  270.2 0.9 multiply_reduce_fusion.2
  271.1 0.6 add_bitcast_fusion.x_ref
  271.7 7.8 exchange.6
  279.4 0.9 reshape_reshape.3
  280.3 0.9 copy.88
  281.2 1.3 copy.65.lse_ref
  282.5 0.7 copy.92
  283.2 1.3 copy.66.w_ref
  284.6 1.4 copy.67.y_ref
  285.9 0.7 reshape.237.lse_ref
  286.6 1.3 constant_dynamic-slice_fusion.3
  287.9 1.3 constant_dynamic-slice_fusion.2
  289.2 1.6 pad_maximum_fusion.z_ref
  290.9 131.9 %table_grad.1 = (f32[3072,960]{1,0:T(8,128)}, f32[1,16384]{1,0:T(1,128)}) custom-call(s32[1]{0:T(128)} %bitcast.23.base_ref, f32[3072,16384]{1,0:T(8,128)} %get-tuple-element.45.lt_ref, bf16[16384,960]{1,0:T(8,128)(2,1)} %get-tuple-element.46.z_ref, f32[1,16384]{1,0:T(1,128)} %reshape.237.lse_ref, f32[1,16384]{1,0:T(1,128)} %reshape.228.w_ref, ...), custom_call_target="tpu_custom_call" | custom-call | flops 96636764160 | bytes 201326592 | tf_op jit(solution)/shard_map/table_grad/pallas_call | solution.py:107
  422.8 0.7 reshape.242.code_ref
  423.5 1.6 multiply_reduce_fusion
  425.1 0.6 broadcast_in_dim.76
  426.3 0.6 multiply_reduce_fusion.1
  426.9 29.3 %place_rows.1 = (bf16[1024,1024]{1,0:T(8,128)(2,1)}, bf16[1024,1024]{1,0:T(8,128)(2,1)}) custom-call(s32[16]{0:T(128)} %reduce_sum.161.count_ref, s32[8,2,1024]{2,1,0:T(2,128)} %bitcast.126, bf16[24576,960]{1,0:T(8,128)(2,1)} %all-gather.8.cloned.1.call-done.e_ref), custom_call_target="tpu_custom_call" | custom-call | flops 10000000000 | bytes 47185920 | tf_op jit(solution)/shard_map/place_rows/pallas_call | solution.py:238
  456.2 120.9 %hidden_grad.3 = f32[1024,1024]{1,0:T(8,128)} custom-call(s32[1]{0:T(128)} %bitcast.25.base_ref, bf16[1024,960]{1,0:T(8,128)(2,1)} %pad_maximum_fusion.z_ref, bf16[24576,960]{1,0:T(8,128)(2,1)} %all-gather.8.cloned.1.call-done.e_ref, f32[2048,1]{1,0:T(8,128)} %copy.65.lse_ref, f32[2048,1]{1,0:T(8,128)} %copy.66.w_ref, s32[2048,1]{1,0:T(8,128)} %copy.67.y_ref), custom_call_target="tpu_custom_call" | custom-call | flops 96636764160 | bytes 47185920 | tf_op jit(solution)/shard_map/hidden_grad/pallas_call | solution.py:146
  577.2 2.0 collective-permute-start
  579.2 120.7 %hidden_grad.2 = f32[1024,1024]{1,0:T(8,128)} custom-call(s32[1]{0:T(128)} %bitcast.25.base_ref, bf16[1024,960]{1,0:T(8,128)(2,1)} %copy-done.2, bf16[24576,960]{1,0:T(8,128)(2,1)} %all-gather.8.cloned.1.call-done.e_ref, f32[2048,1]{1,0:T(8,128)} %copy.65.lse_ref, f32[2048,1]{1,0:T(8,128)} %copy.66.w_ref, s32[2048,1]{1,0:T(8,128)} %copy.67.y_ref), custom_call_target="tpu_custom_call" | custom-call | flops 96636764160 | bytes 47185920 | tf_op jit(solution)/shard_map/hidden_grad/pallas_call | solution.py:146
  699.9 36.2 %add_rows.1 = f32[3072,960]{1,0:T(8,128)} custom-call(s32[16]{0:T(128)} %get-tuple-element.57.count_ref, s32[16,1,1024]{2,1,0:T(1,128)} %reshape.242.code_ref, bf16[16384,960]{1,0:T(8,128)(2,1)} %bitcast.116, f32[3072,960]{1,0:T(8,128)} %get-tuple-element.59.grad_ref), custom_call_target="tpu_custom_call" | custom-call | flops 10000000000 | bytes 31457280 | tf_op jit(solution)/shard_map/add_rows/pallas_call | solution.py:184
  736.2 12.3 %copy.74 = f32[3072,960]{0,1:T(8,128)} copy(f32[3072,960]{1,0:T(8,128)} %add_rows.1) | data formatting | bytes 23592960
  748.4 1.3 copy-done.3
  749.8 4.0 fusion.15
  753.8 3.9 copy.72
  757.7 5.8 fusion.11
  763.7 0.7 maximum_maximum_fusion
  764.3 7.0 exchange.7
  771.3 0.7 reduce_sum.168
  773.2 3.4 fusion.31
  776.9 2.4 copy.73
  (91 shorter events, 7.0 us)
Async XLA Ops:
  7.2 100.5 %all-gather.6.cloned.1.call-start = ((), (), s32[]{:S(2)}) async-start(), calls=%async_computation | async-start | bytes 17825792 | tf_op jit(solution)/shard_map/all_gather | solution.py:359
  25.9 2.7 copy-start
  26.3 4.0 copy-start.10
  27.0 0.6 copy-start.16
  27.1 3.2 copy-start.14
  27.7 2.6 copy-start.12
  28.7 2.0 copy-start.2
  30.6 155.9 %all-gather.10.cloned.1.call-start = ((), (), s32[]{:S(2)}) async-start(), calls=%async_computation.2 | async-start | bytes 17825792 | tf_op jit(solution)/shard_map/all_gather | solution.py:359
  31.4 395.5 %all-gather.8.cloned.1.call-start = ((), (), s32[]{:S(2)}) async-start(), calls=%async_computation.1 | async-start | bytes 56623104 | tf_op jit(solution)/shard_map/all_gather | solution.py:385
  40.0 1.5 copy-start.4
  40.0 659.9 %all-gather.12.cloned.1.call-start = ((), (), s32[]{:S(2)}) async-start(), calls=%async_computation.3 | async-start | bytes 35651584 | tf_op jit(solution)/shard_map/all_gather | solution.py:402
  45.5 133.2 %copy-start.5 = (f32[16,1024]{1,0:T(8,128)}, f32[16,1024]{1,0:T(8,128)S(1)}, u32[]{:S(2)}) copy-start(f32[16,1024]{1,0:T(8,128)S(1)} %get-tuple-element.91) | copy-start | bytes 196612
  186.6 71.3 %copy-start.19 = (f32[1,8192]{1,0:T(1,128)S(1)}, f32[1,8192]{1,0:T(1,128)}, u32[]{:S(2)}) copy-start(f32[1,8192]{1,0:T(1,128)} %get-tuple-element.39) | copy-start | bytes 98308
  186.6 72.2 %copy-start.18 = (f32[1,8192]{1,0:T(1,128)S(1)}, f32[1,8192]{1,0:T(1,128)}, u32[]{:S(2)}) copy-start(f32[1,8192]{1,0:T(1,128)} %get-tuple-element.43) | copy-start | bytes 98308
  290.9 132.0 %copy-start.8 = (s32[16,1024]{1,0:T(8,128)S(1)}, s32[16,1024]{1,0:T(8,128)}, u32[]{:S(2)}) copy-start(s32[16,1024]{1,0:T(8,128)} %select_reduce_fusion.1) | copy-start | bytes 196612
  290.9 132.6 %copy-start.9 = (f32[1,16384]{1,0:T(1,128)S(1)}, f32[1,16384]{1,0:T(1,128)}, u32[]{:S(2)}) copy-start(f32[1,16384]{1,0:T(1,128)} %reshape.228.w_ref) | copy-start | bytes 196612
  290.9 135.4 %copy-start.6 = (f32[16,1024]{1,0:T(8,128)S(1)}, f32[16,1024]{1,0:T(8,128)}, u32[]{:S(2)}) copy-start(f32[16,1024]{1,0:T(8,128)} %copy-done.5) | copy-start | bytes 196612
  290.9 135.4 %copy-start.7 = (f32[16,8,128]{2,1,0:T(8,128)S(1)}, f32[16,8,128]{2,1,0:T(8,128)}, u32[]{:S(2)}) copy-start(f32[16,8,128]{2,1,0:T(8,128)} %exchange.6) | copy-start | bytes 196612
  577.2 180.5 %collective-permute-start.1 = (f32[1024,1024]{1,0:T(8,128)}, f32[1024,1024]{1,0:T(8,128)}, u32[]{:S(2)}, u32[]{:S(2)}) collective-permute-start(f32[1024,1024]{1,0:T(8,128)} %hidden_grad.3), channel_id=1, source_target_pairs={{0,8},{1,9},{2,10},{3,11},{4,12},{5,13},{6,14},{7,15},{8,0},{9,1},... | collective-permute-start | bytes 12582920 | tf_op jit(solution)/shard_map/ppermute | solution.py:395
  577.2 171.3 %collective-permute-start = (bf16[1024,1024]{1,0:T(8,128)(2,1)}, bf16[1024,1024]{1,0:T(8,128)(2,1)S(1)}, u32[]{:S(2)}, u32[]{:S(2)}) collective-permute-start(bf16[1024,1024]{1,0:T(8,128)(2,1)} %get-tuple-element.37), channel_id=1, source_target_pairs={{0,8},{1,9},{2,10},{3,11},{4,12},{5,13},{6,14},{7,15},{8,0},{9,1},... | collective-permute-start | bytes 6291464 | tf_op jit(solution)/shard_map/ppermute | solution.py:398
  736.2 13.6 %copy-start.20 = (pred[1024]{0:T(1024)(128)(4,1)S(1)}, pred[1024]{0:T(1024)(128)(4,1)}, u32[]{:S(2)}) copy-start(pred[1024]{0:T(1024)(128)(4,1)} %fusion.28) | copy-start | bytes 3076
  748.4 1.3 copy-start.3
  749.7 7.9 %copy-start.1 = (bf16[1,1024,960]{2,1,0:T(8,128)(2,1)S(1)}, bf16[1,1024,960]{2,1,0:T(8,128)(2,1)}, u32[]{:S(2)}) copy-start(bf16[1,1024,960]{2,1,0:T(8,128)(2,1)} %copy-done) | copy-start | bytes 5898244
  749.7 8.0 %copy-start.11 = (f32[1024]{0:T(1024)S(1)}, f32[1024]{0:T(1024)}, u32[]{:S(2)}) copy-start(f32[1024]{0:T(1024)} %copy-done.10) | copy-start | bytes 12292
  749.7 8.0 %copy-start.13 = (f32[960]{0:T(1024)S(1)}, f32[960]{0:T(1024)}, u32[]{:S(2)}) copy-start(f32[960]{0:T(1024)} %copy-done.12) | copy-start | bytes 11524
  749.7 8.0 %copy-start.15 = (f32[1024]{0:T(1024)S(1)}, f32[1024]{0:T(1024)}, u32[]{:S(2)}) copy-start(f32[1024]{0:T(1024)} %copy-done.14) | copy-start | bytes 12292
  757.7 6.0 copy-start.21
  764.3 8.9 %copy-start.17 = (f32[1024]{0:T(1024)S(1)}, f32[1024]{0:T(1024)}, u32[]{:S(2)}) copy-start(f32[1024]{0:T(1024)} %copy-done.16) | copy-start | bytes 12292
Sparse Core Ops, SparseCore 0:
  30.8 76.8 all-gather.5
  110.5 76.0 all-gather.9
  189.0 229.8 all-gather.7
  421.0 131.2 all-gather.11
